TPU v7x, 32 devices: a whole 2x2x4 slice. The times are simulated.
32 devices in a mesh: seq: 8 (over z, x), batch: 4 (over y, core).
Axes of the slice: x: 2, y: 2, z: 4, core: 2. Of those that a mesh axis runs over, the one named last changes fastest.
Arguments:
- tokens: bfloat16 [4, 2048, 256], P('batch', 'seq'), may hold values from -6 to 6
- out_grad: bfloat16 [4, 2048, 256], P('batch', 'seq'), may hold values from -6 to 6
- in_weight: bfloat16 [256, 768], replicated, may hold values from -0.375 to 0.375
- out_weight: bfloat16 [256, 256], replicated, may hold values from -0.375 to 0.375
- skip_bias: float32 [256], replicated, may hold values from -4 to 4
- embed_weight: float32 [5, 64], replicated, may hold values from -4 to 4
- embed_bias: float32 [64], replicated, may hold values from -4 to 4
- hidden_weight: float32 [64, 64], replicated, may hold values from -0.75 to 0.75
- hidden_bias: float32 [64], replicated, may hold values from -4 to 4
- filter_weight: float32 [64, 256], replicated, may hold values from -0.75 to 0.75
- sine_freq: float32 [2, 64], replicated, may hold values from 0.5 to 3
- decay_rate: float32 [256], replicated, may hold values from 0.0014990234 to 0.0074951174
Outputs:
- grad_tokens: bfloat16 [4, 2048, 256], P('batch', 'seq')
- grad_in_weight: float32 [256, 768], replicated
- grad_out_weight: float32 [256, 256], replicated
- grad_skip_bias: float32 [256], replicated
- grad_embed_weight: float32 [5, 64], replicated
- grad_embed_bias: float32 [64], replicated
- grad_hidden_weight: float32 [64, 64], replicated
- grad_hidden_bias: float32 [64], replicated
- grad_filter_weight: float32 [64, 256], replicated
- grad_sine_freq: float32 [2, 64], replicated
All inputs are finite; a program needn't handle non-finite values.
Results may differ from a plain program's by a relative error of at most 0.013.
Values may be sent and summed in bfloat16 or wider, within the bound.
A program may use at most 64 MiB of HBM per device.

v0:
```python
import functools
import math

import jax
import jax.numpy as jnp
import numpy as np
from jax import lax
from jax.experimental import pallas as pl
from jax.experimental.pallas import tpu as pltpu
from jax.sharding import PartitionSpec as P

highest = lax.Precision.HIGHEST
MESH = pl.DeviceIdType.MESH
LANES = 128
VMEM_BYTES = 66 * 1000 * 1000


def factor(length):
    total = 2 * length
    first_len = 2
    while first_len * first_len < total and total % (2 * first_len) == 0:
        first_len = first_len * 2
    return first_len, total // first_len


def make_tables(length):
    total = 2 * length
    first_len, second_len = factor(length)
    half = first_len // 2
    kept = half + 1
    pad = -(-kept // 8) * 8
    k1 = np.arange(kept)[None, :, None]
    n1 = np.arange(half)[None, None, :]
    n2 = np.arange(second_len)[:, None, None]
    angle = 2.0 * np.pi * ((k1 * (n1 * second_len + n2)) % total) / total
    fwd = np.zeros((second_len, 2 * pad, half), np.float32)
    fwd[:, :kept] = np.cos(angle)
    fwd[:, pad : pad + kept] = -np.sin(angle)
    weight = np.where((k1 == 0) | (k1 == half), 1.0, 2.0) / total
    inv = np.zeros((second_len, half, 2 * pad), np.float32)
    inv[:, :, :kept] = np.swapaxes(weight * np.cos(angle), 1, 2)
    inv[:, :, pad : pad + kept] = np.swapaxes(-weight * np.sin(angle), 1, 2)
    index = np.arange(second_len)
    small = 2.0 * np.pi * ((index[:, None] * index[None, :]) % second_len) / second_len
    cos, sin = np.cos(small), np.sin(small)
    inner = np.block([[cos, sin], [-sin, cos]])
    outer = np.block([[cos, -sin], [sin, cos]])
    return tuple(jnp.asarray(t, jnp.bfloat16) for t in (fwd, inv, inner, outer))


def lane_roll(value, shift):
    shift = shift % LANES
    return value if shift == 0 else pltpu.roll(value, shift, 1)


def dot_as(left, right, dims):
    return lax.dot_general(
        left,
        right,
        ((dims[:1], dims[1:]), ((), ())),
        precision=highest,
        preferred_element_type=jnp.float32,
    )


def step_kernel(
    axis_n,
    batch_n,
    chan,
    scale,
    tok,
    og,
    inw,
    outw,
    embed,
    embed_raw,
    embed_b,
    hidden_b,
    freqs,
    hidden_w,
    filter_w,
    decay_in,
    skip_in,
    fwd,
    inv,
    inner,
    outer,
    gt_out,
    a_out,
    b_out,
    send_one,
    recv_one,
    send_two,
    recv_two,
    gates,
    x_buf,
    y_out,
    z_buf,
    v_buf,
    net,
    conv_buf,
    sems,
    pk_out,
    extra,
    embed_w,
    vectors,
    *sum_scratch,
):
    n = axis_n
    me = lax.axis_index("seq")
    pos, width = tok.shape
    rows = send_one.shape[1]
    fold = pos // rows
    step = 2 * chan
    second_len, double_pad, half = fwd.shape
    pad = double_pad // 2
    kept = half + 1
    f32, bf16 = jnp.float32, jnp.bfloat16

    barrier = pltpu.get_barrier_semaphore()
    for axis, own_at, count in (("seq", me, n), ("batch", lax.axis_index("batch"), batch_n)):
        for k in range(1, count):
            pl.semaphore_signal(
                barrier, inc=1, device_id={axis: lax.rem(own_at + k, count)}, device_id_type=MESH
            )

    proj = jnp.dot(tok[...], inw[...], preferred_element_type=f32)
    gate_out = proj[:, :width].astype(bf16)
    gate_in = proj[:, width : 2 * width].astype(bf16)
    values = proj[:, 2 * width :].astype(bf16)
    gated_grad = lax.dot_general(
        og[...], outw[...], (((1,), (1,)), ((), ())), preferred_element_type=f32
    ).astype(bf16)
    gates[0] = gate_out
    gates[1] = gate_in
    gates[2] = values
    gates[3] = gated_grad
    mixed = (values.astype(f32) * gate_in.astype(f32)).astype(bf16).astype(f32)
    grad = (gated_grad.astype(f32) * gate_out.astype(f32)).astype(bf16).astype(f32)
    bias_sum = jnp.sum(mixed * grad, axis=0, keepdims=True) * scale

    lane = lax.broadcasted_iota(jnp.int32, (rows, LANES), 1)
    lane_full = lax.broadcasted_iota(jnp.int32, (pos, LANES), 1)
    for d in range(n):
        tile, off = (d * chan) // LANES * LANES, (d * chan) % LANES
        both = jnp.where(
            lane_full < chan,
            lane_roll(mixed[:, tile : tile + LANES], -off),
            lane_roll(grad[:, tile : tile + LANES], chan - off),
        )
        packed = both[:rows]
        for j in range(1, fold):
            packed = jnp.where(
                lane >= j * step, lane_roll(both[j * rows : (j + 1) * rows], j * step), packed
            )
        send_one[d] = packed.astype(bf16)

    pl.semaphore_wait(barrier, n + batch_n - 2)

    def copy(send, recv, which, k):
        dest = lax.rem(me + k, n)
        return pltpu.make_async_remote_copy(
            src_ref=send.at[dest],
            dst_ref=recv.at[me],
            send_sem=sems.at[2 * which, k],
            recv_sem=sems.at[2 * which + 1, k],
            device_id={"seq": dest},
            device_id_type=MESH,
        )

    for k in range(1, n):
        copy(send_one, recv_one, 0, k).start()
    recv_one[me] = send_one[me]
    v_buf[...] = jnp.zeros_like(v_buf)
    extra[...] = jnp.zeros_like(extra)
    length = x_buf.shape[0]
    hid = hidden_w.shape[0]
    tiles = width // LANES

    def select_own(value, target):
        lane_v = lax.broadcasted_iota(jnp.int32, (value.shape[0], LANES), 1)
        got = jnp.zeros((value.shape[0], LANES), f32)
        for i in range(n):
            tile, off = (i * chan) // LANES * LANES, (i * chan) % LANES
            part = lane_roll(value[:, tile : tile + LANES], target - off)
            got = jnp.where(jnp.logical_and(me == i, lane_v >= 0), part, got)
        return jnp.where((lane_v >= target) & (lane_v < target + chan), got, 0.0)

    weight = select_own(filter_w[...], step)
    decay = select_own(decay_in[...], step)
    skip = select_own(skip_in[...], 0) + select_own(skip_in[...], chan)
    inputs = embed_raw.shape[0]
    embed_w[...] = jnp.zeros_like(embed_w)
    embed_w[0:inputs, :] = embed_raw[...]
    embed_w[inputs : inputs + 1, :] = embed_b[...]
    vectors[...] = jnp.zeros_like(vectors)
    vectors[0:2, :] = freqs[...]
    vectors[2:3, :] = hidden_b[...]
    eye = (
        lax.broadcasted_iota(jnp.int32, (8, 8), 0) == lax.broadcasted_iota(jnp.int32, (8, 8), 1)
    ).astype(f32)
    columns = dot_as(vectors[...], eye, (0, 0))
    freq_one, freq_two = columns[:, 0:1], columns[:, 1:2]
    tile_rows = min(256, length)

    def modulation(at_row):
        time = (lax.broadcasted_iota(jnp.int32, (tile_rows, LANES), 0) + at_row).astype(f32)
        return jnp.exp(-decay * time) * (4.0 / math.sqrt(length))

    def net_forward(i, _):
        at = pl.ds(pl.multiple_of(i * tile_rows, tile_rows), tile_rows)
        pre_one = dot_as(embed_w[...], embed[:, at], (0, 0))
        act_one, cos_one = sine_cosine(freq_one * pre_one)
        pre_two = dot_as(hidden_w[...], act_one, (0, 0)) + columns[:, 2:3]
        act_two, cos_two = sine_cosine(freq_two * pre_two)
        net[0, :, at] = pre_one
        net[1, :, at] = act_one
        net[2, :, at] = cos_one
        net[3, :, at] = pre_two
        net[4, :, at] = act_two
        net[5, :, at] = cos_two
        y_out[at, :] = dot_as(act_two, weight, (0, 0)) * modulation(i * tile_rows)
        return 0

    lax.fori_loop(0, length // tile_rows, net_forward, 0)
    for k in range(1, n):
        copy(send_one, recv_one, 0, k).wait()

    for s in range(n):
        block = recv_one[s].astype(f32)
        for j in range(fold):
            at = pl.ds(s * pos + j * rows, rows)
            x_buf[at, :] = jnp.where(lane < step, lane_roll(block, -j * step), y_out[at, :])

    def stage_one(n2, _):
        part = x_buf[pl.ds(n2, half, stride=second_len), :].astype(bf16)
        z_buf[pl.ds(pl.multiple_of(n2 * double_pad, 8), double_pad), :] = jnp.dot(
            fwd[n2], part, preferred_element_type=f32
        )
        return 0

    lax.fori_loop(0, second_len, stage_one, 0, unroll=16)

    lane_k = lax.broadcasted_iota(jnp.int32, (second_len, LANES), 1)
    low = lane_k < step
    mid = (lane_k >= chan) & (lane_k < step)
    sign = jnp.where((lane_k >= chan), -1.0, 1.0).astype(f32)

    def stage_two(k1, _):
        stacked = jnp.concatenate(
            [
                z_buf[pl.ds(k1, second_len, stride=double_pad), :],
                z_buf[pl.ds(pad + k1, second_len, stride=double_pad), :],
            ],
            axis=0,
        ).astype(bf16)
        spec = jnp.dot(inner[...], stacked, preferred_element_type=f32)
        re, im = spec[:second_len], spec[second_len:]
        left_re = jnp.where(low, re, lane_roll(re, chan))
        left_im = jnp.where(low, im, lane_roll(im, chan))
        right_re = jnp.where(mid, lane_roll(re, -chan), lane_roll(re, -step))
        right_im = jnp.where(mid, lane_roll(im, -chan), lane_roll(im, -step)) * sign
        corr_re = jnp.where(lane_k < step, right_re, lane_roll(re, step))
        corr_im = jnp.where(lane_k < step, right_im, lane_roll(im, step) * sign)
        out = jnp.concatenate(
            [
                left_re * corr_re - left_im * corr_im,
                left_re * corr_im + left_im * corr_re,
            ],
            axis=0,
        ).astype(bf16)
        back = jnp.dot(outer[...], out, preferred_element_type=f32)
        v_buf[pl.ds(k1, second_len, stride=double_pad), :] = back[:second_len]
        v_buf[pl.ds(pad + k1, second_len, stride=double_pad), :] = back[second_len:]
        return 0

    unroll = 11 if kept % 11 == 0 else 3 if kept % 3 == 0 else 5 if kept % 5 == 0 else 1
    lax.fori_loop(0, kept, stage_two, 0, unroll=unroll)

    def stage_three(n2, _):
        part = v_buf[pl.ds(pl.multiple_of(n2 * double_pad, 8), double_pad), :].astype(bf16)
        at = pl.ds(n2, half, stride=second_len)
        y_out[at, :] = (
            jnp.dot(inv[n2], part, preferred_element_type=f32) + skip * x_buf[at, :]
        )
        return 0

    lax.fori_loop(0, second_len, stage_three, 0, unroll=16)

    for d in range(n):
        packed = y_out[pl.ds(d * pos, rows), :]
        for j in range(1, fold):
            packed = jnp.where(
                lane >= j * step,
                lane_roll(y_out[pl.ds(d * pos + j * rows, rows), :], j * step),
                packed,
            )
        send_two[d] = packed.astype(bf16)
    for k in range(1, n):
        copy(send_two, recv_two, 1, k).start()
    recv_two[me] = send_two[me]

    lane_t = lax.broadcasted_iota(jnp.int32, (tile_rows, LANES), 1)
    owned = (lane_t >= step) & (lane_t < step + chan)

    def net_backward(i, carry):
        at = pl.ds(pl.multiple_of(i * tile_rows, tile_rows), tile_rows)
        grad_kernel = jnp.where(owned, y_out[at, :], 0.0) * modulation(i * tile_rows)
        grad_weight = dot_as(net[4, :, at], grad_kernel, (1, 0))
        grad_act_two = dot_as(weight, grad_kernel, (1, 1)) * net[5, :, at]
        grad_pre_two = grad_act_two * freq_two
        grad_hidden = dot_as(net[1, :, at], grad_pre_two, (1, 1))
        grad_act_one = dot_as(hidden_w[...], grad_pre_two, (1, 0)) * net[2, :, at]
        grad_pre_one = grad_act_one * freq_one
        rows_at = embed[:, at]
        new = (
            grad_weight,
            grad_hidden,
            dot_as(rows_at, grad_pre_one, (1, 1)),
            dot_as(rows_at, grad_pre_two, (1, 1)),
            dot_as(rows_at, grad_act_one * net[0, :, at], (1, 1)),
            dot_as(rows_at, grad_act_two * net[3, :, at], (1, 1)),
        )
        return tuple(old + term for old, term in zip(carry, new))

    zeros = lambda r, c: jnp.zeros((r, c), f32)
    em = embed.shape[0]
    sums = lax.fori_loop(
        0,
        length // tile_rows,
        net_backward,
        (zeros(hid, LANES), zeros(hid, hid)) + (zeros(em, hid),) * 4,
    )
    sums = tuple(term * (scale * 0.25) for term in sums)
    lane_h = lax.broadcasted_iota(jnp.int32, (hid, LANES), 1)
    for tile in range(tiles):
        placed = zeros(hid, LANES)
        for i in range(n):
            if (i * chan) // LANES == tile:
                off = (i * chan) % LANES
                mask = (lane_h >= off) & (lane_h < off + chan) & (me == i)
                placed = jnp.where(mask, lane_roll(sums[0], off - step), placed)
        extra[tile * hid : (tile + 1) * hid, :] = placed
    base = tiles * hid
    extra[base : base + hid, 0:hid] = sums[1]
    base += hid
    for term in sums[2:]:
        extra[base : base + em, 0:hid] = term
        base += em
    for tile in range(tiles):
        extra[base + tile : base + tile + 1, :] = bias_sum[:, tile * LANES : (tile + 1) * LANES]

    main_sum = make_sum(n, batch_n, pk_out, a_out, sum_scratch[:5], 0)
    extra_sum = make_sum(n, batch_n, extra, b_out, sum_scratch[5:], 1)
    extra_sum.start(0)
    for k in range(1, n):
        copy(send_two, recv_two, 1, k).wait()

    per_tile = LANES // chan
    for tile in range(width // LANES):
        for j in range(fold):
            conv_acc = jnp.zeros((rows, LANES), f32)
            grad_acc = jnp.zeros((rows, LANES), f32)
            for i in range(per_tile):
                block = recv_two[tile * per_tile + i].astype(f32)
                own = (lane >= i * chan) & (lane < (i + 1) * chan)
                conv_acc = jnp.where(own, lane_roll(block, i * chan - j * step), conv_acc)
                grad_acc = jnp.where(own, lane_roll(block, i * chan - j * step - chan), grad_acc)
            at = pl.ds(j * rows, rows)
            conv_buf[0, at, tile * LANES : (tile + 1) * LANES] = conv_acc
            conv_buf[1, at, tile * LANES : (tile + 1) * LANES] = grad_acc

    conv = conv_buf[0]
    grad_mixed = conv_buf[1]
    gated = (gates[0].astype(f32) * conv).astype(bf16)
    grad_proj = jnp.concatenate(
        [
            (gates[3].astype(f32) * conv).astype(bf16),
            (grad_mixed * gates[2].astype(f32)).astype(bf16),
            (grad_mixed * gates[1].astype(f32)).astype(bf16),
        ],
        axis=1,
    )
    first = (((0,), (0,)), ((), ()))
    grad_in = lax.dot_general(tok[...], grad_proj, first, preferred_element_type=f32) * scale
    grad_out = lax.dot_general(gated, og[...], first, preferred_element_type=f32) * scale
    at = 0
    for block in (grad_in, grad_out):
        for j in range(block.shape[1] // LANES):
            pk_out[at : at + width, :] = block[:, j * LANES : (j + 1) * LANES].astype(bf16)
            at += width
    main_sum.start(0)
    gt_out[...] = lax.dot_general(
        grad_proj, inw[...], (((1,), (1,)), ((), ())), preferred_element_type=f32
    ).astype(bf16)
    for phase in range(4):
        for stream in (extra_sum, main_sum):
            stream.finish(phase)
            if phase < 3:
                stream.start(phase + 1)
            else:
                stream.out[...] = stream.whole[...]


class make_sum:
    def __init__(self, ns, nb, src, out, scratch, which):
        self.ns, self.nb, self.src, self.out, self.which = ns, nb, src, out, which
        self.got, self.part, self.got_two, self.whole, self.sems = scratch
        self.me_s, self.me_b = lax.axis_index("seq"), lax.axis_index("batch")
        self.unit = 16 if src.dtype == jnp.bfloat16 else 8
        self.long, self.short = self.got.shape[1], self.got_two.shape[1]

    def rows(self, start, size):
        return pl.ds(pl.multiple_of(start, self.unit), size)

    def copies(self, phase):
        axis, me, n = (
            ("seq", self.me_s, self.ns) if phase in (1, 2) else ("batch", self.me_b, self.nb)
        )
        made = []
        for k in range(1, n):
            dest = lax.rem(me + k, n)
            if phase == 0:
                src, dst = self.src.at[self.rows(dest * self.long, self.long)], self.got.at[k - 1]
            elif phase == 1:
                src = self.part.at[self.rows(dest * self.short, self.short)]
                dst = self.got_two.at[k - 1]
            else:
                start, size = self.me_b * self.long, self.long
                if phase == 2:
                    start, size = start + self.me_s * self.short, self.short
                src = dst = self.whole.at[self.rows(start, size)]
            made.append(
                pltpu.make_async_remote_copy(
                    src_ref=src,
                    dst_ref=dst,
                    send_sem=self.sems.at[phase, 0, k],
                    recv_sem=self.sems.at[phase, 1, k],
                    device_id={axis: dest},
                    device_id_type=MESH,
                )
            )
        return made

    def start(self, phase):
        for item in self.copies(phase):
            item.start()

    def finish(self, phase):
        for item in self.copies(phase):
            item.wait()
        if phase == 0:
            total = self.src[self.rows(self.me_b * self.long, self.long), :].astype(jnp.float32)
            for k in range(1, self.nb):
                total = total + self.got[k - 1].astype(jnp.float32)
            self.part[...] = total.astype(self.part.dtype)
        if phase == 1:
            total = self.part[self.rows(self.me_s * self.short, self.short), :].astype(jnp.float32)
            for k in range(1, self.ns):
                total = total + self.got_two[k - 1].astype(jnp.float32)
            start = self.me_b * self.long + self.me_s * self.short
            self.whole[self.rows(start, self.short), :] = total.astype(self.whole.dtype)


def unpack_kernel(main, extra, g_in, g_out, skip, emb, emb_b, hidden, hidden_b, filt, freq):
    width = g_out.shape[0]
    hid = hidden.shape[0]
    at = 0
    for ref in (g_in, g_out):
        for j in range(ref.shape[1] // LANES):
            ref[:, j * LANES : (j + 1) * LANES] = main[at : at + width, :].astype(jnp.float32)
            at += width
    tiles = width // LANES
    for j in range(tiles):
        filt[:, j * LANES : (j + 1) * LANES] = extra[j * hid : (j + 1) * hid, :]
    base = tiles * hid
    hidden[...] = extra[base : base + hid, 0:hid]
    base += hid
    count = emb.shape[0]
    em = -(-(count + 1) // 8) * 8
    emb[...] = extra[base : base + count, 0:hid]
    emb_b[...] = extra[base + count : base + count + 1, 0:hid]
    hidden_b[...] = extra[base + em + count : base + em + count + 1, 0:hid]
    freq[0:1, :] = extra[base + 2 * em + count : base + 2 * em + count + 1, 0:hid]
    freq[1:2, :] = extra[base + 3 * em + count : base + 3 * em + count + 1, 0:hid]
    base += 4 * em
    for j in range(tiles):
        skip[:, j * LANES : (j + 1) * LANES] = extra[base + j : base + j + 1, :]


def vmem(count):
    return [pl.BlockSpec(memory_space=pltpu.VMEM)] * count


def sine_cosine(angle):
    turns = jnp.round(angle * (1.0 / (2.0 * math.pi)))
    reduced = angle - turns * 6.28125
    reduced = reduced - turns * 0.0019350051879882812
    reduced = reduced - turns * 3.0199157663146e-07
    half = reduced * 0.5
    square = half * half
    sin = half * (
        1.0
        + square
        * (-1.0 / 6 + square * (1.0 / 120 + square * (-1.0 / 5040 + square * (1.0 / 362880 - square / 39916800.0))))
    )
    cos = 1.0 + square * (
        -0.5
        + square
        * (1.0 / 24 + square * (-1.0 / 720 + square * (1.0 / 40320 + square * (-1.0 / 3628800 + square / 479001600.0))))
    )
    return 2.0 * sin * cos, 1.0 - 2.0 * sin * sin


def embedding(length, count):
    rows = np.zeros((-(-(count + 1) // 8) * 8, length), np.float32)
    scaled = np.arange(length) / length
    rows[0] = scaled
    for band_index in range(1, (count - 1) // 2 + 1):
        rows[2 * band_index - 1] = np.cos(2.0 * np.pi * band_index * scaled)
        rows[2 * band_index] = np.sin(2.0 * np.pi * band_index * scaled)
    rows[count] = 1.0
    return jnp.asarray(rows)


def shards(
    tokens,
    out_grad,
    in_weight,
    out_weight,
    skip_bias,
    embed_weight,
    embed_bias,
    hidden_weight,
    hidden_bias,
    filter_weight,
    sine_freq,
    decay_rate,
):
    f32, bf16 = jnp.float32, jnp.bfloat16
    tok, og = tokens[0], out_grad[0]
    pos, width = tok.shape
    ns, nb = lax.axis_size("seq"), lax.axis_size("batch")
    length = pos * ns
    chan = width // ns
    hid = hidden_weight.shape[0]
    count = embed_weight.shape[0]
    embed = embedding(length, count)
    em = embed.shape[0]

    fwd, inv, inner, outer = make_tables(length)
    second_len, double_pad, half = fwd.shape
    rows = pos // (LANES // (2 * chan))
    tiles = width // LANES
    unit = ns * nb * 16
    main_rows = -(-4 * width * tiles // unit) * unit
    unit = ns * nb * 8
    extra_rows = -(-(tiles * hid + hid + 4 * em + tiles) // unit) * unit
    pair = (ns, rows, LANES)
    spectral = (second_len * double_pad, LANES)
    scratch = []
    for total, kind in ((main_rows, bf16), (extra_rows, f32)):
        scratch += [
            pltpu.VMEM((nb - 1, total // nb, LANES), kind),
            pltpu.VMEM((total // nb, LANES), kind),
            pltpu.VMEM((ns - 1, total // nb // ns, LANES), kind),
            pltpu.VMEM((total, LANES), kind),
            pltpu.SemaphoreType.DMA((4, 2, max(ns, nb))),
        ]
    grad_tokens, main, extra = pl.pallas_call(
        functools.partial(step_kernel, ns, nb, chan, 1.0 / math.sqrt(nb * length)),
        out_shape=(
            jax.ShapeDtypeStruct((pos, width), bf16),
            jax.ShapeDtypeStruct((main_rows, LANES), bf16),
            jax.ShapeDtypeStruct((extra_rows, LANES), f32),
        ),
        in_specs=vmem(17),
        out_specs=tuple(vmem(3)),
        scratch_shapes=[
            pltpu.VMEM(pair, bf16),
            pltpu.VMEM(pair, bf16),
            pltpu.VMEM(pair, bf16),
            pltpu.VMEM(pair, bf16),
            pltpu.VMEM((4, pos, width), bf16),
            pltpu.VMEM((length, LANES), f32),
            pltpu.VMEM((length, LANES), f32),
            pltpu.VMEM(spectral, f32),
            pltpu.VMEM(spectral, f32),
            pltpu.VMEM((6, hid, length), f32),
            pltpu.VMEM((2, pos, width), f32),
            pltpu.SemaphoreType.DMA((4, ns)),
            pltpu.VMEM((main_rows, LANES), bf16),
            pltpu.VMEM((extra_rows, LANES), f32),
            pltpu.VMEM((em, hid), f32),
            pltpu.VMEM((8, hid), f32),
        ]
        + scratch,
        compiler_params=pltpu.CompilerParams(
            collective_id=0, has_side_effects=True, vmem_limit_bytes=VMEM_BYTES
        ),
        name="step",
    )(
        tok,
        og,
        in_weight,
        out_weight,
        embed,
        embed_weight,
        embed_bias[None],
        hidden_bias[None],
        sine_freq,
        hidden_weight,
        filter_weight,
        decay_rate[None],
        skip_bias[None],
        fwd,
        inv,
        inner,
        outer,
    )

    shapes = (
        (width, 3 * width),
        (width, width),
        (1, width),
        (count, hid),
        (1, hid),
        (hid, hid),
        (1, hid),
        (hid, width),
        (2, hid),
    )
    out = pl.pallas_call(
        unpack_kernel,
        out_shape=tuple(jax.ShapeDtypeStruct(shape, f32) for shape in shapes),
        in_specs=vmem(2),
        out_specs=tuple(vmem(len(shapes))),
        name="unpack",
    )(main, extra)
    return (
        grad_tokens[None],
        out[0],
        out[1],
        out[2][0],
        out[3],
        out[4][0],
        out[5],
        out[6][0],
        out[7],
        out[8],
    )


def solution(mesh):
    batched = P("batch", "seq", None)
    return jax.shard_map(
        shards,
        mesh=mesh,
        in_specs=(batched, batched) + (P(),) * 10,
        out_specs=(batched,) + (P(),) * 9,
        check_vma=False,
    )
```

profile of v0, /device:TPU:0, one launch (start us, length us, event | category | flops | bytes accessed | tf_op | source)
XLA Modules:
  0.0 61.3 jit_solution(8992996704111118530)
XLA Ops:
  0.6 57.0 %step.1 = (bf16[256,256]{1,0:T(8,128)(2,1)}, bf16[2048,128]{1,0:T(8,128)(2,1)}, f32[256,128]{1,0:T(8,128)}) custom-call(bf16[256,256]{1,0:T(8,128)(2,1)} %bitcast.10, bf16[256,256]{1,0:T(8,128)(2,1)} %bitcast.11, bf16[256,768]{1,0:T(8,128)(2,1)} %inw.1, bf16[256,256]{1,0:T(8,128)(2,1)} %outw.1, f32[8,2048]{1,0:T(8,128)} %constant.10.clone.embed, ...), custom_call_target="tpu_custom_call" | custom-call | tf_op jit(solution)/shard_map/step/pallas_call | solution.py:570
  57.6 2.1 %unpack.1 = (f32[256,768]{1,0:T(8,128)}, f32[256,256]{1,0:T(8,128)}, f32[1,256]{1,0:T(1,128)}, f32[5,64]{1,0:T(8,128)}, f32[1,64]{1,0:T(1,128)}, /*index=5*/f32[...) custom-call(bf16[2048,128]{1,0:T(8,128)(2,1)} %get-tuple-element.23.main, ...), custom_call_target="tpu_custom_call" | custom-call | tf_op jit(solution)/shard_map/unpack/pallas_call | solution.py:633
  59.7 1.6 %copy.28 = bf16[1,256,256]{2,1,0:T(8,128)(2,1)} copy(bf16[1,256,256]{2,1,0:T(8,128)(2,1)} %bitcast.12) | data formatting | bytes 262144
where the time goes:
time: 62.2 us; the launch traced here: 61.3 us
  Pallas kernels  59.1 us (95%)
  local copies, waits for them, and re-layouts  1.57 us (3%)
  between operations  0.66 us (1%)
    pallas_call x1, Pallas kernels, shards(): pl.pallas_call(functools.partial(step_kernel, ns, nb, chan, 1.0 / math.sq...  57 us
    pallas_call x1, Pallas kernels, shards(): pl.pallas_call(unpack_kernel, out_shape=tuple((jax.ShapeDtypeStruct(shape...  2.11 us
    unnamed x1, local copies, waits for them, and re-layouts  1.57 us

commit v1 on v0

--- a/solution.py
+++ b/solution.py
@@ -68,11 +68,15 @@
     batch_n,
     chan,
     scale,
-    tok,
-    og,
-    inw,
-    outw,
-    embed,
+    tok_hbm,
+    og_hbm,
+    inw_hbm,
+    outw_hbm,
+    embed_hbm,
+    fwd_hbm,
+    inv_hbm,
+    inner_hbm,
+    outer_hbm,
     embed_raw,
     embed_b,
     hidden_b,
@@ -81,13 +85,19 @@
     filter_w,
     decay_in,
     skip_in,
+    gt_out,
+    a_out,
+    b_out,
+    tok,
+    og,
+    inw,
+    outw,
+    embed,
     fwd,
     inv,
     inner,
     outer,
-    gt_out,
-    a_out,
-    b_out,
+    load_sems,
     send_one,
     recv_one,
     send_two,
@@ -98,8 +108,13 @@
     z_buf,
     v_buf,
     net,
+    filt_pk,
+    send_grad,
+    grad_pk,
+    modul,
     conv_buf,
     sems,
+    net_sems,
     pk_out,
     extra,
     embed_w,
@@ -108,6 +123,7 @@
 ):
     n = axis_n
     me = lax.axis_index("seq")
+    me_b = lax.axis_index("batch")
     pos, width = tok.shape
     rows = send_one.shape[1]
     fold = pos // rows
@@ -118,11 +134,34 @@
     f32, bf16 = jnp.float32, jnp.bfloat16
 
     barrier = pltpu.get_barrier_semaphore()
-    for axis, own_at, count in (("seq", me, n), ("batch", lax.axis_index("batch"), batch_n)):
+    for axis, own_at, count in (("seq", me, n), ("batch", me_b, batch_n)):
         for k in range(1, count):
             pl.semaphore_signal(
                 barrier, inc=1, device_id={axis: lax.rem(own_at + k, count)}, device_id_type=MESH
             )
+
+    quarter = embed.shape[1]
+    own_part = pl.ds(pl.multiple_of(me_b * quarter, LANES), quarter)
+    loads = [
+        pltpu.make_async_copy(src, dst, load_sems.at[i])
+        for i, (src, dst) in enumerate(
+            (
+                (tok_hbm, tok),
+                (inw_hbm, inw),
+                (og_hbm, og),
+                (outw_hbm, outw),
+                (embed_hbm.at[:, own_part], embed),
+                (fwd_hbm, fwd),
+                (inner_hbm, inner),
+                (outer_hbm, outer),
+                (inv_hbm, inv),
+            )
+        )
+    ]
+    for item in loads:
+        item.start()
+    for item in loads[:4]:
+        item.wait()
 
     proj = jnp.dot(tok[...], inw[...], preferred_element_type=f32)
     gate_out = proj[:, :width].astype(bf16)
@@ -186,8 +225,13 @@
             got = jnp.where(jnp.logical_and(me == i, lane_v >= 0), part, got)
         return jnp.where((lane_v >= target) & (lane_v < target + chan), got, 0.0)
 
-    weight = select_own(filter_w[...], step)
-    decay = select_own(decay_in[...], step)
+    parts = LANES // chan
+    sub = quarter // parts
+    weight = select_own(filter_w[...], 0)
+    decay_own = select_own(decay_in[...], 0)
+    decay = decay_own
+    for j in range(1, parts):
+        decay = decay + lane_roll(decay_own, j * chan)
     skip = select_own(skip_in[...], 0) + select_own(skip_in[...], chan)
     inputs = embed_raw.shape[0]
     embed_w[...] = jnp.zeros_like(embed_w)
@@ -201,14 +245,11 @@
     ).astype(f32)
     columns = dot_as(vectors[...], eye, (0, 0))
     freq_one, freq_two = columns[:, 0:1], columns[:, 1:2]
-    tile_rows = min(256, length)
-
-    def modulation(at_row):
-        time = (lax.broadcasted_iota(jnp.int32, (tile_rows, LANES), 0) + at_row).astype(f32)
-        return jnp.exp(-decay * time) * (4.0 / math.sqrt(length))
+    tile = min(256, quarter)
+    loads[4].wait()
 
     def net_forward(i, _):
-        at = pl.ds(pl.multiple_of(i * tile_rows, tile_rows), tile_rows)
+        at = pl.ds(pl.multiple_of(i * tile, LANES), tile)
         pre_one = dot_as(embed_w[...], embed[:, at], (0, 0))
         act_one, cos_one = sine_cosine(freq_one * pre_one)
         pre_two = dot_as(hidden_w[...], act_one, (0, 0)) + columns[:, 2:3]
@@ -219,18 +260,51 @@
         net[3, :, at] = pre_two
         net[4, :, at] = act_two
         net[5, :, at] = cos_two
-        y_out[at, :] = dot_as(act_two, weight, (0, 0)) * modulation(i * tile_rows)
         return 0
 
-    lax.fori_loop(0, length // tile_rows, net_forward, 0)
+    lax.fori_loop(0, quarter // tile, net_forward, 0, unroll=2 if quarter // tile % 2 == 0 else 1)
+    lane_s = lax.broadcasted_iota(jnp.int32, (sub, LANES), 1)
+    time = lax.broadcasted_iota(jnp.int32, (sub, LANES), 0) + me_b * quarter
+    for j in range(1, parts):
+        time = time + jnp.where(lane_s >= j * chan, sub, 0)
+    modul[...] = jnp.exp(-decay * time.astype(f32)) * (4.0 / math.sqrt(length))
+    packed_filt = jnp.zeros((sub, LANES), f32)
+    for j in range(parts):
+        packed_filt = packed_filt + dot_as(
+            net[4, :, j * sub : (j + 1) * sub], lane_roll(weight, j * chan), (0, 0)
+        )
+    filt_pk[me_b] = (packed_filt * modul[...]).astype(bf16)
+
+    def share(which, k):
+        dest = lax.rem(me_b + k, batch_n)
+        return pltpu.make_async_remote_copy(
+            src_ref=filt_pk.at[me_b] if which == 0 else send_grad.at[dest],
+            dst_ref=filt_pk.at[me_b] if which == 0 else grad_pk.at[me_b],
+            send_sem=net_sems.at[2 * which, k],
+            recv_sem=net_sems.at[2 * which + 1, k],
+            device_id={"batch": dest},
+            device_id_type=MESH,
+        )
+
+    for k in range(1, batch_n):
+        share(0, k).start()
     for k in range(1, n):
         copy(send_one, recv_one, 0, k).wait()
+    for k in range(1, batch_n):
+        share(0, k).wait()
 
     for s in range(n):
         block = recv_one[s].astype(f32)
         for j in range(fold):
-            at = pl.ds(s * pos + j * rows, rows)
-            x_buf[at, :] = jnp.where(lane < step, lane_roll(block, -j * step), y_out[at, :])
+            start = s * pos + j * rows
+            q, rest = start // quarter, start % quarter
+            p, row = rest // sub, rest % sub
+            filt = lane_roll(filt_pk[q, row : row + rows, :].astype(f32), step - p * chan)
+            x_buf[pl.ds(start, rows), :] = jnp.where(
+                lane < step, lane_roll(block, -j * step), filt
+            )
+    for item in loads[5:]:
+        item.wait()
 
     def stage_one(n2, _):
         part = x_buf[pl.ds(n2, half, stride=second_len), :].astype(bf16)
@@ -300,36 +374,57 @@
         copy(send_two, recv_two, 1, k).start()
     recv_two[me] = send_two[me]
 
-    lane_t = lax.broadcasted_iota(jnp.int32, (tile_rows, LANES), 1)
-    owned = (lane_t >= step) & (lane_t < step + chan)
+    owned = [(lane_s >= j * chan) & (lane_s < (j + 1) * chan) for j in range(parts)]
+    for q in range(batch_n):
+        packed = jnp.zeros((sub, LANES), f32)
+        for j in range(parts):
+            part = y_out[pl.ds(q * quarter + j * sub, sub), :]
+            packed = jnp.where(owned[j], lane_roll(part, j * chan - step), packed)
+        send_grad[q] = packed.astype(bf16)
+    for k in range(1, batch_n):
+        share(1, k).start()
+    grad_pk[me_b] = send_grad[me_b]
+    for k in range(1, batch_n):
+        share(1, k).wait()
+    total = grad_pk[0].astype(f32)
+    for q in range(1, batch_n):
+        total = total + grad_pk[q].astype(f32)
+    grad_kernel = total * modul[...]
+
+    em = embed.shape[0]
+    lane_w = lax.broadcasted_iota(jnp.int32, (hid, LANES), 1)
+    grad_weight = jnp.zeros((hid, LANES), f32)
+    for j in range(parts):
+        at = slice(j * sub, (j + 1) * sub)
+        got = dot_as(net[4, :, at], grad_kernel, (1, 0))
+        grad_weight = grad_weight + lane_roll(
+            jnp.where((lane_w >= j * chan) & (lane_w < (j + 1) * chan), got, 0.0), -j * chan
+        )
+        net[5, :, at] = dot_as(lane_roll(weight, j * chan), grad_kernel, (1, 1)) * net[5, :, at]
 
     def net_backward(i, carry):
-        at = pl.ds(pl.multiple_of(i * tile_rows, tile_rows), tile_rows)
-        grad_kernel = jnp.where(owned, y_out[at, :], 0.0) * modulation(i * tile_rows)
-        grad_weight = dot_as(net[4, :, at], grad_kernel, (1, 0))
-        grad_act_two = dot_as(weight, grad_kernel, (1, 1)) * net[5, :, at]
+        at = pl.ds(pl.multiple_of(i * tile, LANES), tile)
+        grad_act_two = net[5, :, at]
         grad_pre_two = grad_act_two * freq_two
         grad_hidden = dot_as(net[1, :, at], grad_pre_two, (1, 1))
         grad_act_one = dot_as(hidden_w[...], grad_pre_two, (1, 0)) * net[2, :, at]
         grad_pre_one = grad_act_one * freq_one
-        rows_at = embed[:, at]
-        new = (
-            grad_weight,
-            grad_hidden,
-            dot_as(rows_at, grad_pre_one, (1, 1)),
-            dot_as(rows_at, grad_pre_two, (1, 1)),
-            dot_as(rows_at, grad_act_one * net[0, :, at], (1, 1)),
-            dot_as(rows_at, grad_act_two * net[3, :, at], (1, 1)),
-        )
-        return tuple(old + term for old, term in zip(carry, new))
+        stacked = jnp.concatenate(
+            [grad_pre_one, grad_pre_two, grad_act_one * net[0, :, at], grad_act_two * net[3, :, at]],
+            axis=0,
+        )
+        return carry[0] + grad_hidden, carry[1] + dot_as(embed[:, at], stacked, (1, 1))
 
     zeros = lambda r, c: jnp.zeros((r, c), f32)
-    em = embed.shape[0]
-    sums = lax.fori_loop(
+    both_sums = lax.fori_loop(
         0,
-        length // tile_rows,
+        quarter // tile,
         net_backward,
-        (zeros(hid, LANES), zeros(hid, hid)) + (zeros(em, hid),) * 4,
+        (zeros(hid, hid), zeros(em, 4 * hid)),
+        unroll=2 if quarter // tile % 2 == 0 else 1,
+    )
+    sums = (grad_weight, both_sums[0]) + tuple(
+        both_sums[1][:, i * hid : (i + 1) * hid] for i in range(4)
     )
     sums = tuple(term * (scale * 0.25) for term in sums)
     lane_h = lax.broadcasted_iota(jnp.int32, (hid, LANES), 1)
@@ -339,7 +434,7 @@
             if (i * chan) // LANES == tile:
                 off = (i * chan) % LANES
                 mask = (lane_h >= off) & (lane_h < off + chan) & (me == i)
-                placed = jnp.where(mask, lane_roll(sums[0], off - step), placed)
+                placed = jnp.where(mask, lane_roll(sums[0], off), placed)
         extra[tile * hid : (tile + 1) * hid, :] = placed
     base = tiles * hid
     extra[base : base + hid, 0:hid] = sums[1]
@@ -462,9 +557,10 @@
             self.whole[self.rows(start, self.short), :] = total.astype(self.whole.dtype)
 
 
-def unpack_kernel(main, extra, g_in, g_out, skip, emb, emb_b, hidden, hidden_b, filt, freq):
+def unpack_kernel(main, extra, tokens_in, tokens_out, g_in, g_out, skip, emb, emb_b, hidden, hidden_b, filt, freq):
     width = g_out.shape[0]
     hid = hidden.shape[0]
+    tokens_out[...] = tokens_in[...]
     at = 0
     for ref in (g_in, g_out):
         for j in range(ref.shape[1] // LANES):
@@ -557,6 +653,7 @@
     unit = ns * nb * 8
     extra_rows = -(-(tiles * hid + hid + 4 * em + tiles) // unit) * unit
     pair = (ns, rows, LANES)
+    shared = (nb, length // nb // (LANES // chan), LANES)
     spectral = (second_len * double_pad, LANES)
     scratch = []
     for total, kind in ((main_rows, bf16), (extra_rows, f32)):
@@ -574,9 +671,19 @@
             jax.ShapeDtypeStruct((main_rows, LANES), bf16),
             jax.ShapeDtypeStruct((extra_rows, LANES), f32),
         ),
-        in_specs=vmem(17),
+        in_specs=[pl.BlockSpec(memory_space=pl.ANY)] * 9 + vmem(8),
         out_specs=tuple(vmem(3)),
         scratch_shapes=[
+            pltpu.VMEM(tok.shape, bf16),
+            pltpu.VMEM(og.shape, bf16),
+            pltpu.VMEM(in_weight.shape, bf16),
+            pltpu.VMEM(out_weight.shape, bf16),
+            pltpu.VMEM((em, length // nb), f32),
+            pltpu.VMEM(fwd.shape, bf16),
+            pltpu.VMEM(inv.shape, bf16),
+            pltpu.VMEM(inner.shape, bf16),
+            pltpu.VMEM(outer.shape, bf16),
+            pltpu.SemaphoreType.DMA((9,)),
             pltpu.VMEM(pair, bf16),
             pltpu.VMEM(pair, bf16),
             pltpu.VMEM(pair, bf16),
@@ -586,9 +693,14 @@
             pltpu.VMEM((length, LANES), f32),
             pltpu.VMEM(spectral, f32),
             pltpu.VMEM(spectral, f32),
-            pltpu.VMEM((6, hid, length), f32),
+            pltpu.VMEM((6, hid, length // nb), f32),
+            pltpu.VMEM(shared, bf16),
+            pltpu.VMEM(shared, bf16),
+            pltpu.VMEM(shared, bf16),
+            pltpu.VMEM(shared[1:], f32),
             pltpu.VMEM((2, pos, width), f32),
             pltpu.SemaphoreType.DMA((4, ns)),
+            pltpu.SemaphoreType.DMA((4, nb)),
             pltpu.VMEM((main_rows, LANES), bf16),
             pltpu.VMEM((extra_rows, LANES), f32),
             pltpu.VMEM((em, hid), f32),
@@ -605,6 +717,10 @@
         in_weight,
         out_weight,
         embed,
+        fwd,
+        inv,
+        inner,
+        outer,
         embed_weight,
         embed_bias[None],
         hidden_bias[None],
@@ -613,10 +729,6 @@
         filter_weight,
         decay_rate[None],
         skip_bias[None],
-        fwd,
-        inv,
-        inner,
-        outer,
     )
 
     shapes = (
@@ -632,22 +744,23 @@
     )
     out = pl.pallas_call(
         unpack_kernel,
-        out_shape=tuple(jax.ShapeDtypeStruct(shape, f32) for shape in shapes),
-        in_specs=vmem(2),
-        out_specs=tuple(vmem(len(shapes))),
+        out_shape=(jax.ShapeDtypeStruct((pos, width), bf16),)
+        + tuple(jax.ShapeDtypeStruct(shape, f32) for shape in shapes),
+        in_specs=vmem(3),
+        out_specs=tuple(vmem(1 + len(shapes))),
         name="unpack",
-    )(main, extra)
+    )(main, extra, grad_tokens)
     return (
-        grad_tokens[None],
-        out[0],
+        out[0][None],
         out[1],
-        out[2][0],
-        out[3],
-        out[4][0],
-        out[5],
-        out[6][0],
-        out[7],
+        out[2],
+        out[3][0],
+        out[4],
+        out[5][0],
+        out[6],
+        out[7][0],
         out[8],
+        out[9],
     )
 
 

time: 62.2 us -> 55.3 us (0.89)
  Pallas kernels: 59.1 us -> 54.3 us
  local copies, waits for them, and re-layouts: 1.57 us -> 0 us
    pallas_call x1, Pallas kernels: 57 us -> 52.1 us  [shards(): pl.pallas_call(functools.partial(step_kernel, ns, nb, chan, 1.0 / math.sq...]
    unnamed x1 -> x0, local copies, waits for them, and re-layouts: 1.57 us -> none
where the time goes in v1:
time: 55.3 us; the launch traced here: 55 us
  Pallas kernels  54.3 us (98%)
  between operations  0.66 us (1%)
    pallas_call x1, Pallas kernels, shards(): pl.pallas_call(functools.partial(step_kernel, ns, nb, chan, 1.0 / math.sq...  52.1 us
    pallas_call x1, Pallas kernels, shards(): pl.pallas_call(unpack_kernel, out_shape=(jax.ShapeDtypeStruct((pos, width...  2.24 us

profile of v1, /device:TPU:0, one launch (start us, length us, event | category | flops | bytes accessed | tf_op | source)
XLA Modules:
  0.0 55.0 jit_solution(7330978446010393590)
XLA Ops:
  0.6 52.1 %step.1 = (bf16[256,256]{1,0:T(8,128)(2,1)}, bf16[2048,128]{1,0:T(8,128)(2,1)}, f32[256,128]{1,0:T(8,128)}) custom-call(bf16[256,256]{1,0:T(8,128)(2,1)} %bitcast.10, bf16[256,256]{1,0:T(8,128)(2,1)} %bitcast.11, bf16[256,768]{1,0:T(8,128)(2,1)} %inw_hbm.1, bf16[256,256]{1,0:T(8,128)(2,1)} %outw_hbm.1, f32[8,2048]{1,0:T(8,128)} %constant.10.clone.embed_hbm, ...), custom_call_target="tpu_custom_call" | custom-call | tf_op jit(solution)/shard_map/step/pallas_call | solution.py:667
  52.8 2.2 %unpack.1 = (bf16[256,256]{1,0:T(8,128)(2,1)}, f32[256,768]{1,0:T(8,128)}, f32[256,256]{1,0:T(8,128)}, f32[1,256]{1,0:T(1,128)}, f32[5,64]{1,0:T(8,128)}, /*inde...) custom-call(bf16[2048,128]{1,0:T(8,128)(2,1)} %get-tuple-element.23.main, ...), custom_call_target="tpu_custom_call" | custom-call | tf_op jit(solution)/shard_map/unpack/pallas_call | solution.py:745

commit v2 on v1

--- a/solution.py
+++ b/solution.py
@@ -77,17 +77,19 @@
     inv_hbm,
     inner_hbm,
     outer_hbm,
-    embed_raw,
-    embed_b,
-    hidden_b,
-    freqs,
-    hidden_w,
-    filter_w,
-    decay_in,
-    skip_in,
+    embed_raw_hbm,
+    embed_b_hbm,
+    hidden_b_hbm,
+    freqs_hbm,
+    hidden_w_hbm,
+    filter_w_hbm,
+    decay_hbm,
+    skip_hbm,
+    gt_hbm,
+    a_hbm,
+    b_hbm,
     gt_out,
-    a_out,
-    b_out,
+    out_sems,
     tok,
     og,
     inw,
@@ -97,6 +99,14 @@
     inv,
     inner,
     outer,
+    embed_raw,
+    embed_b,
+    hidden_b,
+    freqs,
+    hidden_w,
+    filter_w,
+    decay_in,
+    skip_in,
     load_sems,
     send_one,
     recv_one,
@@ -134,11 +144,16 @@
     f32, bf16 = jnp.float32, jnp.bfloat16
 
     barrier = pltpu.get_barrier_semaphore()
-    for axis, own_at, count in (("seq", me, n), ("batch", me_b, batch_n)):
-        for k in range(1, count):
-            pl.semaphore_signal(
-                barrier, inc=1, device_id={axis: lax.rem(own_at + k, count)}, device_id_type=MESH
-            )
+    everyone = n * batch_n
+    own_at = me * batch_n + me_b
+    for k in range(1, everyone):
+        other = lax.rem(own_at + k, everyone)
+        pl.semaphore_signal(
+            barrier,
+            inc=1,
+            device_id={"seq": lax.div(other, batch_n), "batch": lax.rem(other, batch_n)},
+            device_id_type=MESH,
+        )
 
     quarter = embed.shape[1]
     own_part = pl.ds(pl.multiple_of(me_b * quarter, LANES), quarter)
@@ -151,6 +166,14 @@
                 (og_hbm, og),
                 (outw_hbm, outw),
                 (embed_hbm.at[:, own_part], embed),
+                (embed_raw_hbm, embed_raw),
+                (embed_b_hbm, embed_b),
+                (hidden_b_hbm, hidden_b),
+                (freqs_hbm, freqs),
+                (hidden_w_hbm, hidden_w),
+                (filter_w_hbm, filter_w),
+                (decay_hbm, decay_in),
+                (skip_hbm, skip_in),
                 (fwd_hbm, fwd),
                 (inner_hbm, inner),
                 (outer_hbm, outer),
@@ -194,18 +217,29 @@
             )
         send_one[d] = packed.astype(bf16)
 
-    pl.semaphore_wait(barrier, n + batch_n - 2)
+    pl.semaphore_wait(barrier, everyone - 1)
 
     def copy(send, recv, which, k):
         dest = lax.rem(me + k, n)
         return pltpu.make_async_remote_copy(
             src_ref=send.at[dest],
             dst_ref=recv.at[me],
-            send_sem=sems.at[2 * which, k],
-            recv_sem=sems.at[2 * which + 1, k],
+            send_sem=sems.at[2 * which],
+            recv_sem=sems.at[2 * which + 1],
             device_id={"seq": dest},
             device_id_type=MESH,
         )
+
+    def wait_all(send, recv, which):
+        others = pl.ds(0, n - 1)
+        pltpu.make_async_remote_copy(
+            src_ref=send.at[others],
+            dst_ref=recv.at[others],
+            send_sem=sems.at[2 * which],
+            recv_sem=sems.at[2 * which + 1],
+            device_id={"seq": me},
+            device_id_type=MESH,
+        ).wait()
 
     for k in range(1, n):
         copy(send_one, recv_one, 0, k).start()
@@ -227,6 +261,8 @@
 
     parts = LANES // chan
     sub = quarter // parts
+    for item in loads[4:13]:
+        item.wait()
     weight = select_own(filter_w[...], 0)
     decay_own = select_own(decay_in[...], 0)
     decay = decay_own
@@ -246,8 +282,6 @@
     columns = dot_as(vectors[...], eye, (0, 0))
     freq_one, freq_two = columns[:, 0:1], columns[:, 1:2]
     tile = min(256, quarter)
-    loads[4].wait()
-
     def net_forward(i, _):
         at = pl.ds(pl.multiple_of(i * tile, LANES), tile)
         pre_one = dot_as(embed_w[...], embed[:, at], (0, 0))
@@ -280,18 +314,27 @@
         return pltpu.make_async_remote_copy(
             src_ref=filt_pk.at[me_b] if which == 0 else send_grad.at[dest],
             dst_ref=filt_pk.at[me_b] if which == 0 else grad_pk.at[me_b],
-            send_sem=net_sems.at[2 * which, k],
-            recv_sem=net_sems.at[2 * which + 1, k],
+            send_sem=net_sems.at[2 * which],
+            recv_sem=net_sems.at[2 * which + 1],
             device_id={"batch": dest},
             device_id_type=MESH,
         )
 
+    def share_wait(which):
+        others = pl.ds(0, batch_n - 1)
+        pltpu.make_async_remote_copy(
+            src_ref=grad_pk.at[others],
+            dst_ref=grad_pk.at[others],
+            send_sem=net_sems.at[2 * which],
+            recv_sem=net_sems.at[2 * which + 1],
+            device_id={"batch": me_b},
+            device_id_type=MESH,
+        ).wait()
+
     for k in range(1, batch_n):
         share(0, k).start()
-    for k in range(1, n):
-        copy(send_one, recv_one, 0, k).wait()
-    for k in range(1, batch_n):
-        share(0, k).wait()
+    wait_all(send_one, recv_one, 0)
+    share_wait(0)
 
     for s in range(n):
         block = recv_one[s].astype(f32)
@@ -303,7 +346,7 @@
             x_buf[pl.ds(start, rows), :] = jnp.where(
                 lane < step, lane_roll(block, -j * step), filt
             )
-    for item in loads[5:]:
+    for item in loads[13:]:
         item.wait()
 
     def stage_one(n2, _):
@@ -384,8 +427,7 @@
     for k in range(1, batch_n):
         share(1, k).start()
     grad_pk[me_b] = send_grad[me_b]
-    for k in range(1, batch_n):
-        share(1, k).wait()
+    share_wait(1)
     total = grad_pk[0].astype(f32)
     for q in range(1, batch_n):
         total = total + grad_pk[q].astype(f32)
@@ -445,11 +487,12 @@
     for tile in range(tiles):
         extra[base + tile : base + tile + 1, :] = bias_sum[:, tile * LANES : (tile + 1) * LANES]
 
-    main_sum = make_sum(n, batch_n, pk_out, a_out, sum_scratch[:5], 0)
-    extra_sum = make_sum(n, batch_n, extra, b_out, sum_scratch[5:], 1)
-    extra_sum.start(0)
-    for k in range(1, n):
-        copy(send_two, recv_two, 1, k).wait()
+    main_scratch, extra_scratch = sum_scratch[:5], sum_scratch[5:]
+    blocks = main_scratch[1].shape[0]
+    stream = [pair_sum(n, batch_n, pk_out, main_scratch, b) for b in range(blocks)]
+    extra_sum = pair_sum(n, batch_n, extra, extra_scratch, 0)
+    extra_sum.start_pair()
+    wait_all(send_two, recv_two, 1)
 
     per_tile = LANES // chan
     for tile in range(width // LANES):
@@ -477,84 +520,151 @@
         axis=1,
     )
     first = (((0,), (0,)), ((), ()))
-    grad_in = lax.dot_general(tok[...], grad_proj, first, preferred_element_type=f32) * scale
-    grad_out = lax.dot_general(gated, og[...], first, preferred_element_type=f32) * scale
-    at = 0
-    for block in (grad_in, grad_out):
-        for j in range(block.shape[1] // LANES):
+    pieces = [(gated, og[...])] + [
+        (tok[...], grad_proj[:, j * width : (j + 1) * width]) for j in range(3)
+    ]
+    per_block = len(pieces) // blocks if blocks > 1 else len(pieces)
+    for i, (left, right) in enumerate(pieces):
+        block = lax.dot_general(left, right, first, preferred_element_type=f32) * scale
+        for j in range(tiles):
+            at = (i * tiles + j) * width
             pk_out[at : at + width, :] = block[:, j * LANES : (j + 1) * LANES].astype(bf16)
-            at += width
-    main_sum.start(0)
+        if (i + 1) % per_block == 0:
+            done = (i + 1) // per_block - 1
+            stream[done].start_pair()
+            if done == 0:
+                extra_sum.finish_pair()
+                extra_sum.start_scatter()
+            else:
+                stream[done - 1].finish_pair()
+                stream[done - 1].start_scatter()
     gt_out[...] = lax.dot_general(
         grad_proj, inw[...], (((1,), (1,)), ((), ())), preferred_element_type=f32
     ).astype(bf16)
-    for phase in range(4):
-        for stream in (extra_sum, main_sum):
-            stream.finish(phase)
-            if phase < 3:
-                stream.start(phase + 1)
-            else:
-                stream.out[...] = stream.whole[...]
-
-
-class make_sum:
-    def __init__(self, ns, nb, src, out, scratch, which):
-        self.ns, self.nb, self.src, self.out, self.which = ns, nb, src, out, which
-        self.got, self.part, self.got_two, self.whole, self.sems = scratch
-        self.me_s, self.me_b = lax.axis_index("seq"), lax.axis_index("batch")
-        self.unit = 16 if src.dtype == jnp.bfloat16 else 8
-        self.long, self.short = self.got.shape[1], self.got_two.shape[1]
+    stream[-1].finish_pair()
+    stream[-1].start_scatter()
+    outs = [pltpu.make_async_copy(gt_out, gt_hbm, out_sems.at[0])]
+    outs[0].start()
+    every = [extra_sum] + stream
+    for item in every:
+        item.finish_scatter()
+        item.start_gather()
+    for item in every:
+        item.finish_gather()
+        item.start_swap()
+    for i, item in enumerate(every):
+        item.finish_swap()
+        if i == 0:
+            target = b_hbm
+        else:
+            target = a_hbm.at[pl.ds((i - 1) * item.size, item.size), :]
+        outs.append(pltpu.make_async_copy(item.whole, target, out_sems.at[1 + i]))
+        outs[-1].start()
+    for item in outs:
+        item.wait()
+
+
+class pair_sum:
+    def __init__(self, ns, nb, src, scratch, block):
+        got_pair, part, got, whole, sems = (ref.at[block] for ref in scratch)
+        self.got_pair, self.part, self.got, self.whole, self.sems = got_pair, part, got, whole, sems
+        self.src, self.pairs = src, nb // 2
+        me_s, me_b = lax.axis_index("seq"), lax.axis_index("batch")
+        self.core = lax.rem(me_b, 2)
+        self.chips = ns * self.pairs
+        self.own = me_s * self.pairs + lax.div(me_b, 2)
+        self.partner = me_b + 1 - 2 * self.core
+        self.half = part.shape[0]
+        self.size = 2 * self.half
+        self.base = block * self.size
+        self.unit = self.half // self.chips
 
     def rows(self, start, size):
         return pl.ds(pl.multiple_of(start, self.unit), size)
 
-    def copies(self, phase):
-        axis, me, n = (
-            ("seq", self.me_s, self.ns) if phase in (1, 2) else ("batch", self.me_b, self.nb)
-        )
+    def to_partner(self, which):
+        if which == 0:
+            src = self.src.at[self.rows(self.base + (1 - self.core) * self.half, self.half)]
+            dst = self.got_pair
+        else:
+            src = dst = self.whole.at[self.rows(self.core * self.half, self.half)]
+        return pltpu.make_async_remote_copy(
+            src_ref=src,
+            dst_ref=dst,
+            send_sem=self.sems.at[which, 0, 0],
+            recv_sem=self.sems.at[which, 1, 0],
+            device_id={"batch": self.partner},
+            device_id_type=MESH,
+        )
+
+    def to_chips(self, which):
         made = []
-        for k in range(1, n):
-            dest = lax.rem(me + k, n)
-            if phase == 0:
-                src, dst = self.src.at[self.rows(dest * self.long, self.long)], self.got.at[k - 1]
-            elif phase == 1:
-                src = self.part.at[self.rows(dest * self.short, self.short)]
-                dst = self.got_two.at[k - 1]
+        for k in range(1, self.chips):
+            dest = lax.rem(self.own + k, self.chips)
+            if which == 0:
+                src = self.part.at[self.rows(dest * self.unit, self.unit)]
+                dst = self.got.at[k - 1]
             else:
-                start, size = self.me_b * self.long, self.long
-                if phase == 2:
-                    start, size = start + self.me_s * self.short, self.short
-                src = dst = self.whole.at[self.rows(start, size)]
+                at = self.rows(self.core * self.half + self.own * self.unit, self.unit)
+                src = dst = self.whole.at[at]
             made.append(
                 pltpu.make_async_remote_copy(
                     src_ref=src,
                     dst_ref=dst,
-                    send_sem=self.sems.at[phase, 0, k],
-                    recv_sem=self.sems.at[phase, 1, k],
-                    device_id={axis: dest},
+                    send_sem=self.sems.at[which, 0, 1],
+                    recv_sem=self.sems.at[which, 1, 1],
+                    device_id={
+                        "seq": lax.div(dest, self.pairs),
+                        "batch": 2 * lax.rem(dest, self.pairs) + self.core,
+                    },
                     device_id_type=MESH,
                 )
             )
         return made
 
-    def start(self, phase):
-        for item in self.copies(phase):
+    def wait_chips(self, which):
+        pltpu.make_async_remote_copy(
+            src_ref=self.got,
+            dst_ref=self.got,
+            send_sem=self.sems.at[which, 0, 1],
+            recv_sem=self.sems.at[which, 1, 1],
+            device_id={"batch": self.partner},
+            device_id_type=MESH,
+        ).wait()
+
+    def start_pair(self):
+        self.to_partner(0).start()
+
+    def finish_pair(self):
+        self.to_partner(0).wait()
+        mine = self.src[self.rows(self.base + self.core * self.half, self.half), :]
+        total = mine.astype(jnp.float32) + self.got_pair[...].astype(jnp.float32)
+        self.part[...] = total.astype(self.part.dtype)
+
+    def start_scatter(self):
+        for item in self.to_chips(0):
             item.start()
 
-    def finish(self, phase):
-        for item in self.copies(phase):
-            item.wait()
-        if phase == 0:
-            total = self.src[self.rows(self.me_b * self.long, self.long), :].astype(jnp.float32)
-            for k in range(1, self.nb):
-                total = total + self.got[k - 1].astype(jnp.float32)
-            self.part[...] = total.astype(self.part.dtype)
-        if phase == 1:
-            total = self.part[self.rows(self.me_s * self.short, self.short), :].astype(jnp.float32)
-            for k in range(1, self.ns):
-                total = total + self.got_two[k - 1].astype(jnp.float32)
-            start = self.me_b * self.long + self.me_s * self.short
-            self.whole[self.rows(start, self.short), :] = total.astype(self.whole.dtype)
+    def finish_scatter(self):
+        self.wait_chips(0)
+        total = self.part[self.rows(self.own * self.unit, self.unit), :].astype(jnp.float32)
+        for k in range(1, self.chips):
+            total = total + self.got[k - 1].astype(jnp.float32)
+        at = self.rows(self.core * self.half + self.own * self.unit, self.unit)
+        self.whole[at, :] = total.astype(self.whole.dtype)
+
+    def start_gather(self):
+        for item in self.to_chips(1):
+            item.start()
+
+    def finish_gather(self):
+        self.wait_chips(1)
+
+    def start_swap(self):
+        self.to_partner(1).start()
+
+    def finish_swap(self):
+        self.to_partner(1).wait()
 
 
 def unpack_kernel(main, extra, tokens_in, tokens_out, g_in, g_out, skip, emb, emb_b, hidden, hidden_b, filt, freq):
@@ -562,7 +672,7 @@
     hid = hidden.shape[0]
     tokens_out[...] = tokens_in[...]
     at = 0
-    for ref in (g_in, g_out):
+    for ref in (g_out, g_in):
         for j in range(ref.shape[1] // LANES):
             ref[:, j * LANES : (j + 1) * LANES] = main[at : at + width, :].astype(jnp.float32)
             at += width
@@ -648,21 +758,24 @@
     second_len, double_pad, half = fwd.shape
     rows = pos // (LANES // (2 * chan))
     tiles = width // LANES
-    unit = ns * nb * 16
+    chips = ns * (nb // 2)
+    unit = 2 * chips * 16
     main_rows = -(-4 * width * tiles // unit) * unit
-    unit = ns * nb * 8
+    blocks = max(b for b in (1, 2, 4) if main_rows % (b * unit) == 0)
+    unit = 2 * chips * 8
     extra_rows = -(-(tiles * hid + hid + 4 * em + tiles) // unit) * unit
     pair = (ns, rows, LANES)
     shared = (nb, length // nb // (LANES // chan), LANES)
     spectral = (second_len * double_pad, LANES)
     scratch = []
-    for total, kind in ((main_rows, bf16), (extra_rows, f32)):
+    for total, kind, count_at in ((main_rows, bf16, blocks), (extra_rows, f32, 1)):
+        half_rows = total // count_at // 2
         scratch += [
-            pltpu.VMEM((nb - 1, total // nb, LANES), kind),
-            pltpu.VMEM((total // nb, LANES), kind),
-            pltpu.VMEM((ns - 1, total // nb // ns, LANES), kind),
-            pltpu.VMEM((total, LANES), kind),
-            pltpu.SemaphoreType.DMA((4, 2, max(ns, nb))),
+            pltpu.VMEM((count_at, half_rows, LANES), kind),
+            pltpu.VMEM((count_at, half_rows, LANES), kind),
+            pltpu.VMEM((count_at, chips - 1, half_rows // chips, LANES), kind),
+            pltpu.VMEM((count_at, 2 * half_rows, LANES), kind),
+            pltpu.SemaphoreType.DMA((count_at, 2, 2, 2)),
         ]
     grad_tokens, main, extra = pl.pallas_call(
         functools.partial(step_kernel, ns, nb, chan, 1.0 / math.sqrt(nb * length)),
@@ -671,9 +784,11 @@
             jax.ShapeDtypeStruct((main_rows, LANES), bf16),
             jax.ShapeDtypeStruct((extra_rows, LANES), f32),
         ),
-        in_specs=[pl.BlockSpec(memory_space=pl.ANY)] * 9 + vmem(8),
-        out_specs=tuple(vmem(3)),
+        in_specs=[pl.BlockSpec(memory_space=pl.ANY)] * 17,
+        out_specs=(pl.BlockSpec(memory_space=pl.ANY),) * 3,
         scratch_shapes=[
+            pltpu.VMEM((pos, width), bf16),
+            pltpu.SemaphoreType.DMA((2 + blocks,)),
             pltpu.VMEM(tok.shape, bf16),
             pltpu.VMEM(og.shape, bf16),
             pltpu.VMEM(in_weight.shape, bf16),
@@ -683,7 +798,15 @@
             pltpu.VMEM(inv.shape, bf16),
             pltpu.VMEM(inner.shape, bf16),
             pltpu.VMEM(outer.shape, bf16),
-            pltpu.SemaphoreType.DMA((9,)),
+            pltpu.VMEM(embed_weight.shape, f32),
+            pltpu.VMEM((1, hid), f32),
+            pltpu.VMEM((1, hid), f32),
+            pltpu.VMEM(sine_freq.shape, f32),
+            pltpu.VMEM(hidden_weight.shape, f32),
+            pltpu.VMEM(filter_weight.shape, f32),
+            pltpu.VMEM((1, width), f32),
+            pltpu.VMEM((1, width), f32),
+            pltpu.SemaphoreType.DMA((17,)),
             pltpu.VMEM(pair, bf16),
             pltpu.VMEM(pair, bf16),
             pltpu.VMEM(pair, bf16),
@@ -699,8 +822,8 @@
             pltpu.VMEM(shared, bf16),
             pltpu.VMEM(shared[1:], f32),
             pltpu.VMEM((2, pos, width), f32),
-            pltpu.SemaphoreType.DMA((4, ns)),
-            pltpu.SemaphoreType.DMA((4, nb)),
+            pltpu.SemaphoreType.DMA((4,)),
+            pltpu.SemaphoreType.DMA((4,)),
             pltpu.VMEM((main_rows, LANES), bf16),
             pltpu.VMEM((extra_rows, LANES), f32),
             pltpu.VMEM((em, hid), f32),

time: 55.3 us -> 50.1 us (0.906)
  Pallas kernels: 54.3 us -> 49.3 us
    pallas_call x1, Pallas kernels: 52.1 us -> 47.1 us  [shards(): pl.pallas_call(functools.partial(step_kernel, ns, nb, chan, 1.0 / math.sq...]
where the time goes in v2:
time: 50.1 us; the launch traced here: 50 us
  Pallas kernels  49.3 us (98%)
  between operations  0.66 us (1%)
    pallas_call x1, Pallas kernels, shards(): pl.pallas_call(functools.partial(step_kernel, ns, nb, chan, 1.0 / math.sq...  47.1 us
    pallas_call x1, Pallas kernels, shards(): pl.pallas_call(unpack_kernel, out_shape=(jax.ShapeDtypeStruct((pos, width...  2.24 us

profile of v2, /device:TPU:0, one launch (start us, length us, event | category | flops | bytes accessed | tf_op | source)
XLA Modules:
  0.0 50.0 jit_solution(1317656476956378233)
XLA Ops:
  0.6 47.1 %step.1 = (bf16[256,256]{1,0:T(8,128)(2,1)}, bf16[2048,128]{1,0:T(8,128)(2,1)}, f32[256,128]{1,0:T(8,128)}) custom-call(bf16[256,256]{1,0:T(8,128)(2,1)} %bitcast.10, bf16[256,256]{1,0:T(8,128)(2,1)} %bitcast.11, bf16[256,768]{1,0:T(8,128)(2,1)} %inw_hbm.1, bf16[256,256]{1,0:T(8,128)(2,1)} %outw_hbm.1, f32[8,2048]{1,0:T(8,128)} %constant.10.clone.embed_hbm, ...), custom_call_target="tpu_custom_call" | custom-call | tf_op jit(solution)/shard_map/step/pallas_call | solution.py:780
  47.7 2.2 %unpack.1 = (bf16[256,256]{1,0:T(8,128)(2,1)}, f32[256,768]{1,0:T(8,128)}, f32[256,256]{1,0:T(8,128)}, f32[1,256]{1,0:T(1,128)}, f32[5,64]{1,0:T(8,128)}, /*inde...) custom-call(bf16[2048,128]{1,0:T(8,128)(2,1)} %get-tuple-element.23.main, ...), custom_call_target="tpu_custom_call" | custom-call | tf_op jit(solution)/shard_map/unpack/pallas_call | solution.py:868

commit v3 on v2

--- a/solution.py
+++ b/solution.py
@@ -48,6 +48,30 @@
     return tuple(jnp.asarray(t, jnp.bfloat16) for t in (fwd, inv, inner, outer))
 
 
+def selections(chan, dense):
+    parts = LANES // chan
+    fold = parts // 2
+    if not dense:
+        return tuple(jnp.zeros(s, jnp.bfloat16) for s in ((16, LANES), (1, 16, LANES), (16, LANES)))
+    swap = np.zeros((parts * LANES, parts * LANES), np.float32)
+    place = np.zeros((parts, 2 * LANES, LANES), np.float32)
+    gather = np.zeros((parts * LANES, 3 * LANES), np.float32)
+    c = np.arange(chan)
+    for i in range(parts):
+        for u in range(parts):
+            swap[u * LANES + i * chan + c, i * LANES + u * chan + c] = 1.0
+    for p in range(parts):
+        e, j = p // fold, p % fold
+        place[p, j * chan + c, c] = 1.0
+        place[p, j * chan + c, 3 * chan + c] = 1.0
+        place[p, (fold + j) * chan + c, 2 * chan + c] = 1.0
+        place[p, LANES + p * chan + c, chan + c] = 1.0
+        gather[p * LANES + chan + c, e * LANES + j * chan + c] = 1.0
+        gather[p * LANES + 2 * chan + c, e * LANES + (fold + j) * chan + c] = 1.0
+        gather[p * LANES + 3 * chan + c, 2 * LANES + p * chan + c] = 1.0
+    return tuple(jnp.asarray(t, jnp.bfloat16) for t in (swap, place, gather))
+
+
 def lane_roll(value, shift):
     shift = shift % LANES
     return value if shift == 0 else pltpu.roll(value, shift, 1)
@@ -85,6 +109,9 @@
     filter_w_hbm,
     decay_hbm,
     skip_hbm,
+    swap_hbm,
+    place_hbm,
+    gather_hbm,
     gt_hbm,
     a_hbm,
     b_hbm,
@@ -107,6 +134,9 @@
     filter_w,
     decay_in,
     skip_in,
+    swap,
+    place,
+    gather,
     load_sems,
     send_one,
     recv_one,
@@ -165,6 +195,7 @@
                 (inw_hbm, inw),
                 (og_hbm, og),
                 (outw_hbm, outw),
+                (swap_hbm, swap),
                 (embed_hbm.at[:, own_part], embed),
                 (embed_raw_hbm, embed_raw),
                 (embed_b_hbm, embed_b),
@@ -174,10 +205,12 @@
                 (filter_w_hbm, filter_w),
                 (decay_hbm, decay_in),
                 (skip_hbm, skip_in),
+                (place_hbm, place),
                 (fwd_hbm, fwd),
                 (inner_hbm, inner),
                 (outer_hbm, outer),
                 (inv_hbm, inv),
+                (gather_hbm, gather),
             )
         )
     ]
@@ -202,19 +235,32 @@
     bias_sum = jnp.sum(mixed * grad, axis=0, keepdims=True) * scale
 
     lane = lax.broadcasted_iota(jnp.int32, (rows, LANES), 1)
-    lane_full = lax.broadcasted_iota(jnp.int32, (pos, LANES), 1)
-    for d in range(n):
+    half_lanes = fold * chan
+    parts = LANES // chan
+    tiles = width // LANES
+    dense = swap.shape[0] == parts * LANES
+    loads[4].wait()
+    if dense:
+        for t in range(tiles):
+            at = slice(t * LANES, (t + 1) * LANES)
+            left = jnp.concatenate(
+                [
+                    source[j * rows : (j + 1) * rows, at].astype(bf16)
+                    for source in (mixed, grad)
+                    for j in range(fold)
+                ],
+                axis=1,
+            )
+            packed = jnp.dot(left, swap[...], preferred_element_type=f32).astype(bf16)
+            for i in range(parts):
+                send_one[t * parts + i] = packed[:, i * LANES : (i + 1) * LANES]
+    for d in range(0 if dense else n):
         tile, off = (d * chan) // LANES * LANES, (d * chan) % LANES
-        both = jnp.where(
-            lane_full < chan,
-            lane_roll(mixed[:, tile : tile + LANES], -off),
-            lane_roll(grad[:, tile : tile + LANES], chan - off),
-        )
-        packed = both[:rows]
-        for j in range(1, fold):
-            packed = jnp.where(
-                lane >= j * step, lane_roll(both[j * rows : (j + 1) * rows], j * step), packed
-            )
+        packed = None
+        for i in range(2 * fold):
+            source, j = (mixed, i) if i < fold else (grad, i - fold)
+            part = lane_roll(source[j * rows : (j + 1) * rows, tile : tile + LANES], i * chan - off)
+            packed = part if packed is None else jnp.where(lane >= i * chan, part, packed)
         send_one[d] = packed.astype(bf16)
 
     pl.semaphore_wait(barrier, everyone - 1)
@@ -246,9 +292,10 @@
     recv_one[me] = send_one[me]
     v_buf[...] = jnp.zeros_like(v_buf)
     extra[...] = jnp.zeros_like(extra)
-    length = x_buf.shape[0]
+    length = n * pos
+    group = second_len + 1
+    stride = double_pad + 1
     hid = hidden_w.shape[0]
-    tiles = width // LANES
 
     def select_own(value, target):
         lane_v = lax.broadcasted_iota(jnp.int32, (value.shape[0], LANES), 1)
@@ -259,16 +306,16 @@
             got = jnp.where(jnp.logical_and(me == i, lane_v >= 0), part, got)
         return jnp.where((lane_v >= target) & (lane_v < target + chan), got, 0.0)
 
-    parts = LANES // chan
     sub = quarter // parts
-    for item in loads[4:13]:
+    for item in loads[5:15]:
         item.wait()
     weight = select_own(filter_w[...], 0)
     decay_own = select_own(decay_in[...], 0)
     decay = decay_own
     for j in range(1, parts):
         decay = decay + lane_roll(decay_own, j * chan)
-    skip = select_own(skip_in[...], 0) + select_own(skip_in[...], chan)
+    skip_own = select_own(skip_in[...], chan)
+    skip_other = select_own(skip_in[...], step)
     inputs = embed_raw.shape[0]
     embed_w[...] = jnp.zeros_like(embed_w)
     embed_w[0:inputs, :] = embed_raw[...]
@@ -336,22 +383,45 @@
     wait_all(send_one, recv_one, 0)
     share_wait(0)
 
-    for s in range(n):
-        block = recv_one[s].astype(f32)
+    piece = min(rows, second_len)
+    lane_p = lax.broadcasted_iota(jnp.int32, (piece, LANES), 1)
+
+    def row_of(position):
+        return position // second_len * group + position % second_len
+
+    for block in range(n * fold if dense else 0):
+        q, p = block // parts, block % parts
+        both = jnp.concatenate([recv_one[block // fold], filt_pk[q]], axis=1)
+        placed = jnp.dot(both, place[p], preferred_element_type=f32)
+        for low in range(0, rows, piece):
+            x_buf[pl.ds(row_of(block * rows + low), piece), :] = placed[low : low + piece]
+    for s in range(0 if dense else n):
         for j in range(fold):
-            start = s * pos + j * rows
-            q, rest = start // quarter, start % quarter
-            p, row = rest // sub, rest % sub
-            filt = lane_roll(filt_pk[q, row : row + rows, :].astype(f32), step - p * chan)
-            x_buf[pl.ds(start, rows), :] = jnp.where(
-                lane < step, lane_roll(block, -j * step), filt
-            )
-    for item in loads[13:]:
+            for low in range(0, rows, piece):
+                start = s * pos + j * rows + low
+                q, rest = start // quarter, start % quarter
+                p, row = rest // sub, rest % sub
+                block = recv_one[s, low : low + piece, :].astype(f32)
+                filt = filt_pk[q, row : row + piece, :].astype(f32)
+                x_buf[pl.ds(row_of(start), piece), :] = jnp.where(
+                    lane_p < chan,
+                    lane_roll(block, -j * chan),
+                    jnp.where(
+                        lane_p < step,
+                        lane_roll(filt, (1 - p) * chan),
+                        jnp.where(
+                            lane_p < step + chan,
+                            lane_roll(block, step - half_lanes - j * chan),
+                            lane_roll(block, (3 - j) * chan),
+                        ),
+                    ),
+                )
+    for item in loads[15:]:
         item.wait()
 
     def stage_one(n2, _):
-        part = x_buf[pl.ds(n2, half, stride=second_len), :].astype(bf16)
-        z_buf[pl.ds(pl.multiple_of(n2 * double_pad, 8), double_pad), :] = jnp.dot(
+        part = x_buf[pl.ds(n2, half, stride=group), :].astype(bf16)
+        z_buf[pl.ds(n2 * stride, double_pad), :] = jnp.dot(
             fwd[n2], part, preferred_element_type=f32
         )
         return 0
@@ -359,71 +429,83 @@
     lax.fori_loop(0, second_len, stage_one, 0, unroll=16)
 
     lane_k = lax.broadcasted_iota(jnp.int32, (second_len, LANES), 1)
-    low = lane_k < step
-    mid = (lane_k >= chan) & (lane_k < step)
-    sign = jnp.where((lane_k >= chan), -1.0, 1.0).astype(f32)
+    own_sign = jnp.where((lane_k >= 3 * chan) & (lane_k < 4 * chan), -1.0, 1.0).astype(f32)
+    other_sign = jnp.where((lane_k >= step) & (lane_k < 3 * chan), -1.0, 1.0).astype(f32)
 
     def stage_two(k1, _):
         stacked = jnp.concatenate(
             [
-                z_buf[pl.ds(k1, second_len, stride=double_pad), :],
-                z_buf[pl.ds(pad + k1, second_len, stride=double_pad), :],
+                z_buf[pl.ds(k1, second_len, stride=stride), :],
+                z_buf[pl.ds(pad + k1, second_len, stride=stride), :],
             ],
             axis=0,
         ).astype(bf16)
         spec = jnp.dot(inner[...], stacked, preferred_element_type=f32)
         re, im = spec[:second_len], spec[second_len:]
-        left_re = jnp.where(low, re, lane_roll(re, chan))
-        left_im = jnp.where(low, im, lane_roll(im, chan))
-        right_re = jnp.where(mid, lane_roll(re, -chan), lane_roll(re, -step))
-        right_im = jnp.where(mid, lane_roll(im, -chan), lane_roll(im, -step)) * sign
-        corr_re = jnp.where(lane_k < step, right_re, lane_roll(re, step))
-        corr_im = jnp.where(lane_k < step, right_im, lane_roll(im, step) * sign)
+        other_re = lane_roll(re, chan) + skip_other
+        re = re + skip_own
+        other_im = lane_roll(im, chan) * other_sign
+        im = im * own_sign
         out = jnp.concatenate(
-            [
-                left_re * corr_re - left_im * corr_im,
-                left_re * corr_im + left_im * corr_re,
-            ],
-            axis=0,
+            [re * other_re - im * other_im, re * other_im + im * other_re], axis=0
         ).astype(bf16)
         back = jnp.dot(outer[...], out, preferred_element_type=f32)
-        v_buf[pl.ds(k1, second_len, stride=double_pad), :] = back[:second_len]
-        v_buf[pl.ds(pad + k1, second_len, stride=double_pad), :] = back[second_len:]
+        v_buf[pl.ds(k1, second_len, stride=stride), :] = back[:second_len]
+        v_buf[pl.ds(pad + k1, second_len, stride=stride), :] = back[second_len:]
         return 0
 
     unroll = 11 if kept % 11 == 0 else 3 if kept % 3 == 0 else 5 if kept % 5 == 0 else 1
     lax.fori_loop(0, kept, stage_two, 0, unroll=unroll)
 
     def stage_three(n2, _):
-        part = v_buf[pl.ds(pl.multiple_of(n2 * double_pad, 8), double_pad), :].astype(bf16)
-        at = pl.ds(n2, half, stride=second_len)
-        y_out[at, :] = (
-            jnp.dot(inv[n2], part, preferred_element_type=f32) + skip * x_buf[at, :]
+        part = v_buf[pl.ds(n2 * stride, double_pad), :].astype(bf16)
+        y_out[pl.ds(n2, half, stride=group), :] = jnp.dot(
+            inv[n2], part, preferred_element_type=f32
         )
         return 0
 
     lax.fori_loop(0, second_len, stage_three, 0, unroll=16)
 
-    for d in range(n):
-        packed = y_out[pl.ds(d * pos, rows), :]
-        for j in range(1, fold):
-            packed = jnp.where(
-                lane >= j * step,
-                lane_roll(y_out[pl.ds(d * pos + j * rows, rows), :], j * step),
-                packed,
-            )
-        send_two[d] = packed.astype(bf16)
+    for q in range(batch_n if dense else 0):
+        left = jnp.concatenate(
+            [
+                jnp.concatenate(
+                    [
+                        y_out[pl.ds(row_of((q * parts + p) * rows + low), piece), :]
+                        for low in range(0, rows, piece)
+                    ],
+                    axis=0,
+                ).astype(bf16)
+                for p in range(parts)
+            ],
+            axis=1,
+        )
+        packed = jnp.dot(left, gather[...], preferred_element_type=f32).astype(bf16)
+        send_two[2 * q] = packed[:, :LANES]
+        send_two[2 * q + 1] = packed[:, LANES : 2 * LANES]
+        send_grad[q] = packed[:, 2 * LANES :]
+    for d in range(0 if dense else n):
+        for low in range(0, rows, piece):
+            packed = None
+            for j in range(fold):
+                at = pl.ds(row_of(d * pos + j * rows + low), piece)
+                part = lane_roll(y_out[at, :], j * step - chan)
+                packed = part if j == 0 else jnp.where(lane_p >= j * step, part, packed)
+            send_two[d, low : low + piece, :] = packed.astype(bf16)
     for k in range(1, n):
         copy(send_two, recv_two, 1, k).start()
     recv_two[me] = send_two[me]
 
-    owned = [(lane_s >= j * chan) & (lane_s < (j + 1) * chan) for j in range(parts)]
-    for q in range(batch_n):
-        packed = jnp.zeros((sub, LANES), f32)
-        for j in range(parts):
-            part = y_out[pl.ds(q * quarter + j * sub, sub), :]
-            packed = jnp.where(owned[j], lane_roll(part, j * chan - step), packed)
-        send_grad[q] = packed.astype(bf16)
+    small = min(sub, piece)
+    lane_q = lax.broadcasted_iota(jnp.int32, (small, LANES), 1)
+    for q in range(0 if dense else batch_n):
+        for low in range(0, sub, small):
+            packed = None
+            for j in range(parts):
+                at = pl.ds(row_of(q * quarter + j * sub + low), small)
+                part = lane_roll(y_out[at, :], (j - 3) * chan)
+                packed = part if j == 0 else jnp.where(lane_q >= j * chan, part, packed)
+            send_grad[q, low : low + small, :] = packed.astype(bf16)
     for k in range(1, batch_n):
         share(1, k).start()
     grad_pk[me_b] = send_grad[me_b]
@@ -495,7 +577,14 @@
     wait_all(send_two, recv_two, 1)
 
     per_tile = LANES // chan
-    for tile in range(width // LANES):
+    for t in range(tiles if dense else 0):
+        at = slice(t * LANES, (t + 1) * LANES)
+        left = jnp.concatenate([recv_two[t * parts + i] for i in range(parts)], axis=1)
+        back = jnp.dot(left, swap[...], preferred_element_type=f32)
+        for u in range(parts):
+            j = u % fold
+            conv_buf[u // fold, j * rows : (j + 1) * rows, at] = back[:, u * LANES : (u + 1) * LANES]
+    for tile in range(0 if dense else width // LANES):
         for j in range(fold):
             conv_acc = jnp.zeros((rows, LANES), f32)
             grad_acc = jnp.zeros((rows, LANES), f32)
@@ -758,15 +847,20 @@
     second_len, double_pad, half = fwd.shape
     rows = pos // (LANES // (2 * chan))
     tiles = width // LANES
+    parts = LANES // chan
     chips = ns * (nb // 2)
     unit = 2 * chips * 16
     main_rows = -(-4 * width * tiles // unit) * unit
     blocks = max(b for b in (1, 2, 4) if main_rows % (b * unit) == 0)
     unit = 2 * chips * 8
     extra_rows = -(-(tiles * hid + hid + 4 * em + tiles) // unit) * unit
+    swap, place, gather = selections(
+        chan, second_len <= rows and nb * parts * rows == length and parts * LANES <= 512
+    )
     pair = (ns, rows, LANES)
     shared = (nb, length // nb // (LANES // chan), LANES)
-    spectral = (second_len * double_pad, LANES)
+    spectral = (second_len * (double_pad + 1), LANES)
+    spaced = (half * (second_len + 1), LANES)
     scratch = []
     for total, kind, count_at in ((main_rows, bf16, blocks), (extra_rows, f32, 1)):
         half_rows = total // count_at // 2
@@ -784,7 +878,7 @@
             jax.ShapeDtypeStruct((main_rows, LANES), bf16),
             jax.ShapeDtypeStruct((extra_rows, LANES), f32),
         ),
-        in_specs=[pl.BlockSpec(memory_space=pl.ANY)] * 17,
+        in_specs=[pl.BlockSpec(memory_space=pl.ANY)] * 20,
         out_specs=(pl.BlockSpec(memory_space=pl.ANY),) * 3,
         scratch_shapes=[
             pltpu.VMEM((pos, width), bf16),
@@ -806,14 +900,17 @@
             pltpu.VMEM(filter_weight.shape, f32),
             pltpu.VMEM((1, width), f32),
             pltpu.VMEM((1, width), f32),
-            pltpu.SemaphoreType.DMA((17,)),
+            pltpu.VMEM(swap.shape, bf16),
+            pltpu.VMEM(place.shape, bf16),
+            pltpu.VMEM(gather.shape, bf16),
+            pltpu.SemaphoreType.DMA((20,)),
             pltpu.VMEM(pair, bf16),
             pltpu.VMEM(pair, bf16),
             pltpu.VMEM(pair, bf16),
             pltpu.VMEM(pair, bf16),
             pltpu.VMEM((4, pos, width), bf16),
-            pltpu.VMEM((length, LANES), f32),
-            pltpu.VMEM((length, LANES), f32),
+            pltpu.VMEM(spaced, f32),
+            pltpu.VMEM(spaced, f32),
             pltpu.VMEM(spectral, f32),
             pltpu.VMEM(spectral, f32),
             pltpu.VMEM((6, hid, length // nb), f32),
@@ -852,6 +949,9 @@
         filter_weight,
         decay_rate[None],
         skip_bias[None],
+        swap,
+        place,
+        gather,
     )
 
     shapes = (

time: 50.1 us -> 48.3 us (0.964)
  Pallas kernels: 49.3 us -> 47.5 us
    pallas_call x1, Pallas kernels: 47.1 us -> 45.2 us  [shards(): pl.pallas_call(functools.partial(step_kernel, ns, nb, chan, 1.0 / math.sq...]
where the time goes in v3:
time: 48.3 us; the launch traced here: 48.1 us
  Pallas kernels  47.5 us (98%)
  between operations  0.66 us (1%)
    pallas_call x1, Pallas kernels, shards(): pl.pallas_call(functools.partial(step_kernel, ns, nb, chan, 1.0 / math.sq...  45.2 us
    pallas_call x1, Pallas kernels, shards(): pl.pallas_call(unpack_kernel, out_shape=(jax.ShapeDtypeStruct((pos, width...  2.24 us

profile of v3, /device:TPU:0, one launch (start us, length us, event | category | flops | bytes accessed | tf_op | source)
XLA Modules:
  0.0 48.1 jit_solution(12525406514826047090)
XLA Ops:
  0.6 45.2 %step.1 = (bf16[256,256]{1,0:T(8,128)(2,1)}, bf16[2048,128]{1,0:T(8,128)(2,1)}, f32[256,128]{1,0:T(8,128)}) custom-call(bf16[256,256]{1,0:T(8,128)(2,1)} %bitcast.10, bf16[256,256]{1,0:T(8,128)(2,1)} %bitcast.11, bf16[256,768]{1,0:T(8,128)(2,1)} %inw_hbm.1, bf16[256,256]{1,0:T(8,128)(2,1)} %outw_hbm.1, f32[8,2048]{1,0:T(8,128)} %constant.16.clone.embed_hbm, ...), custom_call_target="tpu_custom_call" | custom-call | tf_op jit(solution)/shard_map/step/pallas_call | solution.py:874
  45.9 2.2 %unpack.1 = (bf16[256,256]{1,0:T(8,128)(2,1)}, f32[256,768]{1,0:T(8,128)}, f32[256,256]{1,0:T(8,128)}, f32[1,256]{1,0:T(1,128)}, f32[5,64]{1,0:T(8,128)}, /*inde...) custom-call(bf16[2048,128]{1,0:T(8,128)(2,1)} %get-tuple-element.23.main, ...), custom_call_target="tpu_custom_call" | custom-call | tf_op jit(solution)/shard_map/unpack/pallas_call | solution.py:968

commit v4 on v3

--- a/solution.py
+++ b/solution.py
@@ -12,6 +12,7 @@
 highest = lax.Precision.HIGHEST
 MESH = pl.DeviceIdType.MESH
 LANES = 128
+BLOCKS = (1, 2)
 VMEM_BYTES = 66 * 1000 * 1000
 
 
@@ -173,18 +174,12 @@
     kept = half + 1
     f32, bf16 = jnp.float32, jnp.bfloat16
 
-    barrier = pltpu.get_barrier_semaphore()
-    everyone = n * batch_n
-    own_at = me * batch_n + me_b
-    for k in range(1, everyone):
-        other = lax.rem(own_at + k, everyone)
-        pl.semaphore_signal(
-            barrier,
-            inc=1,
-            device_id={"seq": lax.div(other, batch_n), "batch": lax.rem(other, batch_n)},
-            device_id_type=MESH,
-        )
-
+    seq_dests = shifted_all(me, n)
+    pairs = batch_n // 2
+    chip_dests = [
+        (dest, lax.div(dest, pairs), 2 * lax.rem(dest, pairs) + lax.rem(me_b, 2))
+        for dest in shifted_all(me * pairs + lax.div(me_b, 2), n * pairs)
+    ]
     quarter = embed.shape[1]
     own_part = pl.ds(pl.multiple_of(me_b * quarter, LANES), quarter)
     loads = [
@@ -216,6 +211,14 @@
     ]
     for item in loads:
         item.start()
+    barrier = pltpu.get_barrier_semaphore()
+    other_core = [
+        lax.rem(me_b + k, batch_n) for k in range(1, batch_n, 2)
+    ]
+    for seq, batch in [dest[1:] for dest in chip_dests] + [(me, peer) for peer in other_core]:
+        pl.semaphore_signal(
+            barrier, inc=1, device_id={"seq": seq, "batch": batch}, device_id_type=MESH
+        )
     for item in loads[:4]:
         item.wait()
 
@@ -232,7 +235,6 @@
     gates[3] = gated_grad
     mixed = (values.astype(f32) * gate_in.astype(f32)).astype(bf16).astype(f32)
     grad = (gated_grad.astype(f32) * gate_out.astype(f32)).astype(bf16).astype(f32)
-    bias_sum = jnp.sum(mixed * grad, axis=0, keepdims=True) * scale
 
     lane = lax.broadcasted_iota(jnp.int32, (rows, LANES), 1)
     half_lanes = fold * chan
@@ -263,10 +265,11 @@
             packed = part if packed is None else jnp.where(lane >= i * chan, part, packed)
         send_one[d] = packed.astype(bf16)
 
-    pl.semaphore_wait(barrier, everyone - 1)
+    pl.semaphore_wait(barrier, len(chip_dests) + len(other_core))
+
 
     def copy(send, recv, which, k):
-        dest = lax.rem(me + k, n)
+        dest = seq_dests[k - 1]
         return pltpu.make_async_remote_copy(
             src_ref=send.at[dest],
             dst_ref=recv.at[me],
@@ -290,6 +293,9 @@
     for k in range(1, n):
         copy(send_one, recv_one, 0, k).start()
     recv_one[me] = send_one[me]
+    mixed = (gates[2].astype(f32) * gates[1].astype(f32)).astype(bf16).astype(f32)
+    grad = (gates[3].astype(f32) * gates[0].astype(f32)).astype(bf16).astype(f32)
+    bias_sum = jnp.sum(mixed * grad, axis=0, keepdims=True) * scale
     v_buf[...] = jnp.zeros_like(v_buf)
     extra[...] = jnp.zeros_like(extra)
     length = n * pos
@@ -571,8 +577,8 @@
 
     main_scratch, extra_scratch = sum_scratch[:5], sum_scratch[5:]
     blocks = main_scratch[1].shape[0]
-    stream = [pair_sum(n, batch_n, pk_out, main_scratch, b) for b in range(blocks)]
-    extra_sum = pair_sum(n, batch_n, extra, extra_scratch, 0)
+    stream = [pair_sum(n, batch_n, pk_out, main_scratch, b, chip_dests) for b in range(blocks)]
+    extra_sum = pair_sum(n, batch_n, extra, extra_scratch, 0, chip_dests)
     extra_sum.start_pair()
     wait_all(send_two, recv_two, 1)
 
@@ -627,34 +633,80 @@
             else:
                 stream[done - 1].finish_pair()
                 stream[done - 1].start_scatter()
+    stream[-1].finish_pair()
+    stream[-1].start_scatter()
+    extra_sum.finish_scatter()
+    extra_sum.start_gather()
     gt_out[...] = lax.dot_general(
         grad_proj, inw[...], (((1,), (1,)), ((), ())), preferred_element_type=f32
     ).astype(bf16)
-    stream[-1].finish_pair()
-    stream[-1].start_scatter()
-    outs = [pltpu.make_async_copy(gt_out, gt_hbm, out_sems.at[0])]
+    outs = [pltpu.make_async_copy(gt_out, gt_hbm, out_sems.at[0, 0])]
     outs[0].start()
-    every = [extra_sum] + stream
-    for item in every:
+    for item in stream:
         item.finish_scatter()
         item.start_gather()
-    for item in every:
+    extra_sum.finish_gather()
+    extra_sum.start_swap()
+
+    def finish(i, item):
+        target, base = (b_hbm, 0) if i == 0 else (a_hbm, (i - 1) * item.size)
+        for side in range(2):
+            core = item.core if side == 0 else 1 - item.core
+            at = item.rows(core * item.half, item.half)
+            to = item.rows(base + core * item.half, item.half)
+            outs.append(
+                pltpu.make_async_copy(item.whole.at[at], target.at[to], out_sems.at[1 + i, side])
+            )
+            if side == 1:
+                item.finish_swap()
+            outs[-1].start()
+
+    finish(0, extra_sum)
+    for item in stream:
         item.finish_gather()
         item.start_swap()
-    for i, item in enumerate(every):
-        item.finish_swap()
-        if i == 0:
-            target = b_hbm
-        else:
-            target = a_hbm.at[pl.ds((i - 1) * item.size, item.size), :]
-        outs.append(pltpu.make_async_copy(item.whole, target, out_sems.at[1 + i]))
-        outs[-1].start()
+    for i, item in enumerate(stream):
+        finish(1 + i, item)
     for item in outs:
         item.wait()
 
 
+def digits_of(count):
+    radices = []
+    while count % 2 == 0 and count > 4 and len(radices) < 2:
+        radices.append(2)
+        count = count // 2
+    return [count] + radices
+
+
+def far_first(count):
+    radices = digits_of(count)
+    moves = [()]
+    for radix in radices:
+        moves = [m + (d,) for m in moves for d in range(radix)]
+    moves = [m for m in moves if any(m)]
+    return sorted(moves, key=lambda m: -2 * min(m[0], radices[0] - m[0]) - sum(m[1:]))
+
+
+def shifted_all(own, count):
+    radices = digits_of(count)
+    below, tables = count, []
+    for radix in radices:
+        below = below // radix
+        digit = lax.rem(lax.div(own, below), radix)
+        tables.append([lax.rem(digit + step, radix) * below for step in range(radix)])
+    made = []
+    for move in far_first(count):
+        total = tables[0][move[0]]
+        for table, step in zip(tables[1:], move[1:]):
+            total = total + table[step]
+        made.append(total)
+    return made
+
+
 class pair_sum:
-    def __init__(self, ns, nb, src, scratch, block):
+    def __init__(self, ns, nb, src, scratch, block, dests):
+        self.dests = dests
         got_pair, part, got, whole, sems = (ref.at[block] for ref in scratch)
         self.got_pair, self.part, self.got, self.whole, self.sems = got_pair, part, got, whole, sems
         self.src, self.pairs = src, nb // 2
@@ -688,11 +740,10 @@
 
     def to_chips(self, which):
         made = []
-        for k in range(1, self.chips):
-            dest = lax.rem(self.own + k, self.chips)
+        for i, (dest, seq, batch) in enumerate(self.dests):
             if which == 0:
                 src = self.part.at[self.rows(dest * self.unit, self.unit)]
-                dst = self.got.at[k - 1]
+                dst = self.got.at[i]
             else:
                 at = self.rows(self.core * self.half + self.own * self.unit, self.unit)
                 src = dst = self.whole.at[at]
@@ -702,10 +753,7 @@
                     dst_ref=dst,
                     send_sem=self.sems.at[which, 0, 1],
                     recv_sem=self.sems.at[which, 1, 1],
-                    device_id={
-                        "seq": lax.div(dest, self.pairs),
-                        "batch": 2 * lax.rem(dest, self.pairs) + self.core,
-                    },
+                    device_id={"seq": seq, "batch": batch},
                     device_id_type=MESH,
                 )
             )
@@ -851,7 +899,7 @@
     chips = ns * (nb // 2)
     unit = 2 * chips * 16
     main_rows = -(-4 * width * tiles // unit) * unit
-    blocks = max(b for b in (1, 2, 4) if main_rows % (b * unit) == 0)
+    blocks = max(b for b in BLOCKS if main_rows % (b * unit) == 0)
     unit = 2 * chips * 8
     extra_rows = -(-(tiles * hid + hid + 4 * em + tiles) // unit) * unit
     swap, place, gather = selections(
@@ -882,7 +930,7 @@
         out_specs=(pl.BlockSpec(memory_space=pl.ANY),) * 3,
         scratch_shapes=[
             pltpu.VMEM((pos, width), bf16),
-            pltpu.SemaphoreType.DMA((2 + blocks,)),
+            pltpu.SemaphoreType.DMA((2 + blocks, 2)),
             pltpu.VMEM(tok.shape, bf16),
             pltpu.VMEM(og.shape, bf16),
             pltpu.VMEM(in_weight.shape, bf16),

time: 48.3 us -> 46.7 us (0.967)
  Pallas kernels: 47.5 us -> 45.9 us
    pallas_call x1, Pallas kernels: 45.2 us -> 43.7 us  [shards(): pl.pallas_call(functools.partial(step_kernel, ns, nb, chan, 1.0 / math.sq...]
where the time goes in v4:
time: 46.7 us; the launch traced here: 46.6 us
  Pallas kernels  45.9 us (98%)
  between operations  0.66 us (1%)
    pallas_call x1, Pallas kernels, shards(): pl.pallas_call(functools.partial(step_kernel, ns, nb, chan, 1.0 / math.sq...  43.7 us
    pallas_call x1, Pallas kernels, shards(): pl.pallas_call(unpack_kernel, out_shape=(jax.ShapeDtypeStruct((pos, width...  2.24 us

profile of v4, /device:TPU:0, one launch (start us, length us, event | category | flops | bytes accessed | tf_op | source)
XLA Modules:
  0.0 46.6 jit_solution(13437160701842008582)
XLA Ops:
  0.6 43.7 %step.1 = (bf16[256,256]{1,0:T(8,128)(2,1)}, bf16[2048,128]{1,0:T(8,128)(2,1)}, f32[256,128]{1,0:T(8,128)}) custom-call(bf16[256,256]{1,0:T(8,128)(2,1)} %bitcast.10, bf16[256,256]{1,0:T(8,128)(2,1)} %bitcast.11, bf16[256,768]{1,0:T(8,128)(2,1)} %inw_hbm.1, bf16[256,256]{1,0:T(8,128)(2,1)} %outw_hbm.1, f32[8,2048]{1,0:T(8,128)} %constant.16.clone.embed_hbm, ...), custom_call_target="tpu_custom_call" | custom-call | tf_op jit(solution)/shard_map/step/pallas_call | solution.py:922
  44.3 2.2 %unpack.1 = (bf16[256,256]{1,0:T(8,128)(2,1)}, f32[256,768]{1,0:T(8,128)}, f32[256,256]{1,0:T(8,128)}, f32[1,256]{1,0:T(1,128)}, f32[5,64]{1,0:T(8,128)}, /*inde...) custom-call(bf16[2048,128]{1,0:T(8,128)(2,1)} %get-tuple-element.23.main, ...), custom_call_target="tpu_custom_call" | custom-call | tf_op jit(solution)/shard_map/unpack/pallas_call | solution.py:1016

commit v5 on v4

--- a/solution.py
+++ b/solution.py
@@ -432,7 +432,7 @@
         )
         return 0
 
-    lax.fori_loop(0, second_len, stage_one, 0, unroll=16)
+    lax.fori_loop(0, second_len, stage_one, 0, unroll=32)
 
     lane_k = lax.broadcasted_iota(jnp.int32, (second_len, LANES), 1)
     own_sign = jnp.where((lane_k >= 3 * chan) & (lane_k < 4 * chan), -1.0, 1.0).astype(f32)
@@ -460,7 +460,7 @@
         v_buf[pl.ds(pad + k1, second_len, stride=stride), :] = back[second_len:]
         return 0
 
-    unroll = 11 if kept % 11 == 0 else 3 if kept % 3 == 0 else 5 if kept % 5 == 0 else 1
+    unroll = 33 if kept == 33 else 13 if kept % 13 == 0 else 3 if kept % 3 == 0 else 5 if kept % 5 == 0 else 1
     lax.fori_loop(0, kept, stage_two, 0, unroll=unroll)
 
     def stage_three(n2, _):
@@ -470,7 +470,7 @@
         )
         return 0
 
-    lax.fori_loop(0, second_len, stage_three, 0, unroll=16)
+    lax.fori_loop(0, second_len, stage_three, 0, unroll=32)
 
     for q in range(batch_n if dense else 0):
         left = jnp.concatenate(

time: 46.7 us -> 45.6 us (0.976)
  Pallas kernels: 45.9 us -> 44.7 us
    pallas_call x1, Pallas kernels: 43.7 us -> 42.5 us  [shards(): pl.pallas_call(functools.partial(step_kernel, ns, nb, chan, 1.0 / math.sq...]
where the time goes in v5:
time: 45.6 us; the launch traced here: 45.4 us
  Pallas kernels  44.7 us (98%)
  between operations  0.66 us (1%)
    pallas_call x1, Pallas kernels, shards(): pl.pallas_call(functools.partial(step_kernel, ns, nb, chan, 1.0 / math.sq...  42.5 us
    pallas_call x1, Pallas kernels, shards(): pl.pallas_call(unpack_kernel, out_shape=(jax.ShapeDtypeStruct((pos, width...  2.24 us

profile of v5, /device:TPU:0, one launch (start us, length us, event | category | flops | bytes accessed | tf_op | source)
XLA Modules:
  0.0 45.4 jit_solution(15035850164581130189)
XLA Ops:
  0.6 42.5 %step.1 = (bf16[256,256]{1,0:T(8,128)(2,1)}, bf16[2048,128]{1,0:T(8,128)(2,1)}, f32[256,128]{1,0:T(8,128)}) custom-call(bf16[256,256]{1,0:T(8,128)(2,1)} %bitcast.10, bf16[256,256]{1,0:T(8,128)(2,1)} %bitcast.11, bf16[256,768]{1,0:T(8,128)(2,1)} %inw_hbm.1, bf16[256,256]{1,0:T(8,128)(2,1)} %outw_hbm.1, f32[8,2048]{1,0:T(8,128)} %constant.16.clone.embed_hbm, ...), custom_call_target="tpu_custom_call" | custom-call | tf_op jit(solution)/shard_map/step/pallas_call | solution.py:922
  43.1 2.2 %unpack.1 = (bf16[256,256]{1,0:T(8,128)(2,1)}, f32[256,768]{1,0:T(8,128)}, f32[256,256]{1,0:T(8,128)}, f32[1,256]{1,0:T(1,128)}, f32[5,64]{1,0:T(8,128)}, /*inde...) custom-call(bf16[2048,128]{1,0:T(8,128)(2,1)} %get-tuple-element.23.main, ...), custom_call_target="tpu_custom_call" | custom-call | tf_op jit(solution)/shard_map/unpack/pallas_call | solution.py:1016

commit v6 on v5

--- a/solution.py
+++ b/solution.py
@@ -117,6 +117,7 @@
     a_hbm,
     b_hbm,
     gt_out,
+    tok_t,
     out_sems,
     tok,
     og,
@@ -219,13 +220,15 @@
         pl.semaphore_signal(
             barrier, inc=1, device_id={"seq": seq, "batch": batch}, device_id_type=MESH
         )
-    for item in loads[:4]:
+    for item in loads[:2]:
         item.wait()
 
     proj = jnp.dot(tok[...], inw[...], preferred_element_type=f32)
     gate_out = proj[:, :width].astype(bf16)
     gate_in = proj[:, width : 2 * width].astype(bf16)
     values = proj[:, 2 * width :].astype(bf16)
+    for item in loads[2:4]:
+        item.wait()
     gated_grad = lax.dot_general(
         og[...], outw[...], (((1,), (1,)), ((), ())), preferred_element_type=f32
     ).astype(bf16)
@@ -293,6 +296,7 @@
     for k in range(1, n):
         copy(send_one, recv_one, 0, k).start()
     recv_one[me] = send_one[me]
+    tok_t[...] = tok[...].T
     mixed = (gates[2].astype(f32) * gates[1].astype(f32)).astype(bf16).astype(f32)
     grad = (gates[3].astype(f32) * gates[0].astype(f32)).astype(bf16).astype(f32)
     bias_sum = jnp.sum(mixed * grad, axis=0, keepdims=True) * scale
@@ -615,12 +619,13 @@
         axis=1,
     )
     first = (((0,), (0,)), ((), ()))
-    pieces = [(gated, og[...])] + [
-        (tok[...], grad_proj[:, j * width : (j + 1) * width]) for j in range(3)
+    pieces = [(gated, og[...], first)] + [
+        (tok_t[...], grad_proj[:, j * width : (j + 1) * width], (((1,), (0,)), ((), ())))
+        for j in range(3)
     ]
     per_block = len(pieces) // blocks if blocks > 1 else len(pieces)
-    for i, (left, right) in enumerate(pieces):
-        block = lax.dot_general(left, right, first, preferred_element_type=f32) * scale
+    for i, (left, right, dims) in enumerate(pieces):
+        block = lax.dot_general(left, right, dims, preferred_element_type=f32) * scale
         for j in range(tiles):
             at = (i * tiles + j) * width
             pk_out[at : at + width, :] = block[:, j * LANES : (j + 1) * LANES].astype(bf16)
@@ -930,6 +935,7 @@
         out_specs=(pl.BlockSpec(memory_space=pl.ANY),) * 3,
         scratch_shapes=[
             pltpu.VMEM((pos, width), bf16),
+            pltpu.VMEM((width, pos), bf16),
             pltpu.SemaphoreType.DMA((2 + blocks, 2)),
             pltpu.VMEM(tok.shape, bf16),
             pltpu.VMEM(og.shape, bf16),

time: 45.6 us -> 45.5 us (level)
  no operation moved by 1% of the time
where the time goes in v6:
time: 45.5 us; the launch traced here: 45.4 us
  Pallas kernels  44.7 us (98%)
  between operations  0.66 us (1%)
    pallas_call x1, Pallas kernels, shards(): pl.pallas_call(functools.partial(step_kernel, ns, nb, chan, 1.0 / math.sq...  42.5 us
    pallas_call x1, Pallas kernels, shards(): pl.pallas_call(unpack_kernel, out_shape=(jax.ShapeDtypeStruct((pos, width...  2.24 us

profile of v6, /device:TPU:0, one launch (start us, length us, event | category | flops | bytes accessed | tf_op | source)
XLA Modules:
  0.0 45.4 jit_solution(1106312031732846486)
XLA Ops:
  0.6 42.5 %step.1 = (bf16[256,256]{1,0:T(8,128)(2,1)}, bf16[2048,128]{1,0:T(8,128)(2,1)}, f32[256,128]{1,0:T(8,128)}) custom-call(bf16[256,256]{1,0:T(8,128)(2,1)} %bitcast.10, bf16[256,256]{1,0:T(8,128)(2,1)} %bitcast.11, bf16[256,768]{1,0:T(8,128)(2,1)} %inw_hbm.1, bf16[256,256]{1,0:T(8,128)(2,1)} %outw_hbm.1, f32[8,2048]{1,0:T(8,128)} %constant.16.clone.embed_hbm, ...), custom_call_target="tpu_custom_call" | custom-call | tf_op jit(solution)/shard_map/step/pallas_call | solution.py:927
  43.1 2.2 %unpack.1 = (bf16[256,256]{1,0:T(8,128)(2,1)}, f32[256,768]{1,0:T(8,128)}, f32[256,256]{1,0:T(8,128)}, f32[1,256]{1,0:T(1,128)}, f32[5,64]{1,0:T(8,128)}, /*inde...) custom-call(bf16[2048,128]{1,0:T(8,128)(2,1)} %get-tuple-element.23.main, ...), custom_call_target="tpu_custom_call" | custom-call | tf_op jit(solution)/shard_map/unpack/pallas_call | solution.py:1022
